TPU v7x, 32 devices: a 4x4x1 block of a 4x4x8 slice. The times are simulated.
32 devices in a mesh: rep: 1 (over z), dp: 32 (over x, y, core).
Axes of the slice: x: 4, y: 4, z: 1, core: 2. Of those that a mesh axis runs over, the one named last changes fastest.
The devices are a block of a 4x4x8 slice.
Arguments:
- x: bfloat16 [32, 2048, 1024], P(('rep', 'dp'))
- dy: bfloat16 [32, 2048, 1024], P(('rep', 'dp'))
- w_gate: bfloat16 [2, 1024, 3200], P(None, 'dp')
- w_up: bfloat16 [2, 1024, 3200], P(None, 'dp')
- w_down: bfloat16 [2, 3200, 1024], P(None, 'dp')
Outputs:
- output 1: bfloat16 [32, 2048, 1024], P(('rep', 'dp'))
- output 2: bfloat16 [2, 1024, 3200], P('rep', 'dp')
- output 3: bfloat16 [2, 1024, 3200], P('rep', 'dp')
- output 4: bfloat16 [2, 3200, 1024], P('rep', 'dp')
All inputs are finite; a program needn't handle non-finite values.
Results may differ from a plain program's by a relative error of at most 0.018.
Values are sent between devices in bfloat16 or wider.
A program may use at most 768 MiB of HBM per device.

v0:
```python
import jax
import jax.numpy as jnp
from jax import lax

NAMES = ("w_gate", "w_up", "w_down")


def matmul(a, w):
    return jnp.dot(a, w, preferred_element_type=jnp.float32).astype(jnp.bfloat16)


def normed(h):
    wide = h.astype(jnp.float32)
    scale = lax.rsqrt(jnp.mean(wide**2, -1, keepdims=True) + 1e-6)
    return (wide * scale).astype(jnp.bfloat16)


def layer(h, w):
    a = normed(h)
    gate = jnp.dot(a, w["w_gate"], preferred_element_type=jnp.float32)
    up = jnp.dot(a, w["w_up"], preferred_element_type=jnp.float32)
    return h + matmul((jax.nn.silu(gate) * up).astype(jnp.bfloat16), w["w_down"])


def stack(weights, h):
    for number in range(weights["w_gate"].shape[0]):
        h = layer(h, {name: w[number] for name, w in weights.items()})
    return h


def solution(mesh):
    groups = mesh.shape["rep"]

    def step(x, dy, *weights):
        shape = x.shape
        x, dy = (t.reshape(groups, -1, *t.shape[1:]) for t in (x, dy))

        def of_a_group(x, dy):
            _, back = jax.vjp(stack, dict(zip(NAMES, weights, strict=True)), x)
            by_weights, by_x = back(dy)
            return (by_x, *(by_weights[name] for name in NAMES))

        by_x, *by_weights = jax.vmap(of_a_group)(x, dy)
        return (by_x.reshape(shape), *(t.reshape(-1, *t.shape[2:]) for t in by_weights))

    return step
```

profile of v0, /device:TPU:97, one launch (start us, length us, event | category | flops | bytes accessed | tf_op | source)
XLA Modules:
  0.0 895.6 jit_solution(6579136475907040525)
XLA Ops:
  15.9 6.5 copy.13
  26.2 6.4 copy.14
  32.6 26.0 %all-gather.30.cloned.1.call-done = bf16[1,1024,3200]{2,1,0:T(8,128)(2,1)} async-done(((bf16[1,32,3200]{2,1,0:T(8,128)(2,1)}), bf16[1,1024,3200]{2,1,0:T(8,128)(2,1)}) %all-gather.30.cloned.1.call-update) | async-done | bytes 6553616 | tf_op jit(solution)/vmap(jvp())/squeeze | solution.py:27
  58.6 22.9 %fusion.61 = f32[2048,3200]{1,0:T(8,128)} fusion(bf16[1,1024,3200]{2,1,0:T(8,128)(2,1)} %all-gather.30.cloned.1.call-done, bf16[1,2048,1024]{1,2,0:T(8,128)(2,1)} %copy.13, f32[2048]{0:T(1024)S(1)} %bitcast.243), kind=kOutput, calls=%fused_computation.80 | convolution fusion | flops 13428064256 | bytes 36970496 | tf_op jit(solution)/vmap(jvp())/dot_general | solution.py:20
  81.5 22.2 %all-gather.32.cloned.1.call-done = bf16[1,1024,3200]{2,1,0:T(8,128)(2,1)} async-done(((bf16[1,32,3200]{2,1,0:T(8,128)(2,1)}), bf16[1,1024,3200]{2,1,0:T(8,128)(2,1)}) %all-gather.32.cloned.1.call-update) | async-done | bytes 6553616 | tf_op jit(solution)/vmap(jvp())/squeeze | solution.py:27
  103.7 23.1 %fusion.57 = f32[2048,3200]{1,0:T(8,128)} fusion(bf16[1,1024,3200]{2,1,0:T(8,128)(2,1)} %all-gather.32.cloned.1.call-done, bf16[1,2048,1024]{1,2,0:T(8,128)(2,1)} %copy.13, f32[2048]{0:T(1024)S(1)} %bitcast.244), kind=kOutput, calls=%fused_computation.76 | convolution fusion | flops 13428064256 | bytes 36970496 | tf_op jit(solution)/vmap(jvp())/dot_general | solution.py:21
  126.8 22.9 %fusion.26 = bf16[2048,3200]{1,0:T(8,128)(2,1)} fusion(f32[2048,3200]{1,0:T(8,128)} %fusion.57, f32[2048,3200]{1,0:T(8,128)} %fusion.61), kind=kLoop, calls=%fused_computation.44 | loop fusion | flops 39321600 | bytes 65536000
  149.7 14.0 %all-gather.34.cloned.1.call-done = bf16[1,3200,1024]{2,0,1:T(2,128)(2,1)} async-done(((bf16[1,100,1024]{2,0,1:T(2,128)(2,1)}), bf16[1,3200,1024]{2,0,1:T(2,128)(2,1)}) %all-gather.34.cloned.1.call-update) | async-done | bytes 6553616 | tf_op jit(solution)/vmap(jvp())/squeeze | solution.py:27
  163.7 22.7 %fusion.41 = (f32[2048]{0:T(1024)S(1)}, bf16[1,2048,1024]{1,2,0:T(8,128)(2,1)}) fusion(bf16[1,2048,1024]{1,2,0:T(8,128)(2,1)} %copy.13, bf16[2048,3200]{1,0:T(8,128)(2,1)} %fusion.26, bf16[1,3200,1024]{2,0,1:T(2,128)(2,1)} %all-gather.34.cloned.1.call-done), kind=kOutput, calls=%fused_computation.60 | convolution fusion | flops 13432256512 | bytes 28057600 | tf_op jit(solution)/vmap(jvp())/dot_general | solution.py:9
  187.1 37.3 %all-gather.38.cloned.1.call-done = bf16[1,3200,1024]{2,0,1:T(2,128)(2,1)} async-done(((bf16[1,100,1024]{2,0,1:T(2,128)(2,1)}), bf16[1,3200,1024]{2,0,1:T(2,128)(2,1)}) %all-gather.38.cloned.1.call-update) | async-done | bytes 6553616 | tf_op jit(solution)/vmap(jvp())/squeeze | solution.py:27
  224.4 22.6 %convolution_convert_fusion.1 = bf16[2048,3200]{1,0:T(8,128)(2,1)} fusion(bf16[1,3200,1024]{2,0,1:T(2,128)(2,1)} %all-gather.38.cloned.1.call-done, bf16[1,2048,1024]{2,1,0:T(8,128)(2,1)} %param), kind=kOutput, calls=%fused_computation.35 | convolution fusion | flops 13428326400 | bytes 23855104 | tf_op jit(solution)/vmap(transpose(jvp()))/dot_general | solution.py:9
  247.0 23.0 %all-gather.36.cloned.1.call-done = bf16[1,1024,3200]{2,1,0:T(8,128)(2,1)} async-done(((bf16[1,32,3200]{2,1,0:T(8,128)(2,1)}), bf16[1,1024,3200]{2,1,0:T(8,128)(2,1)}) %all-gather.36.cloned.1.call-update) | async-done | bytes 6553616 | tf_op jit(solution)/vmap(jvp())/squeeze | solution.py:27
  270.0 23.0 %fusion.54 = f32[2048,3200]{1,0:T(8,128)} fusion(bf16[1,1024,3200]{2,1,0:T(8,128)(2,1)} %all-gather.36.cloned.1.call-done, bf16[1,2048,1024]{1,2,0:T(8,128)(2,1)} %get-tuple-element.19, f32[2048]{0:T(1024)S(1)} %bitcast.248), kind=kOutput, calls=%fused_computation.73 | convolution fusion | flops 13428064256 | bytes 36970496 | tf_op jit(solution)/vmap(jvp())/dot_general | solution.py:20
  293.0 25.6 %fusion.22 = f32[3200,1024]{0,1:T(8,128)} fusion(bf16[2048,3200]{1,0:T(8,128)(2,1)} %convolution_convert_fusion.1, f32[2048,3200]{1,0:T(8,128)} %fusion.54, bf16[1,2048,1024]{1,2,0:T(8,128)(2,1)} %get-tuple-element.19, f32[2048]{0:T(1024)S(1)} %bitcast.249), kind=kOutput, calls=%fused_computation.32 | convolution fusion | flops 13467385856 | bytes 56631296 | tf_op jit(solution)/vmap(transpose(jvp()))/dot_general | solution.py:21
  318.7 23.0 %fusion.49 = f32[2048,3200]{1,0:T(8,128)} fusion(bf16[1,1024,3200]{2,1,0:T(8,128)(2,1)} %all-gather.40.cloned.1.call-done, bf16[1,2048,1024]{1,2,0:T(8,128)(2,1)} %get-tuple-element.19, f32[2048]{0:T(1024)S(1)} %bitcast.250), kind=kOutput, calls=%fused_computation.68 | convolution fusion | flops 13428064256 | bytes 36970496 | tf_op jit(solution)/vmap(jvp())/dot_general | solution.py:21
  341.7 26.8 %fusion.6 = bf16[2048,3200]{1,0:T(8,128)(2,1)} fusion(f32[2048,3200]{1,0:T(8,128)} %fusion.54, f32[2048,3200]{1,0:T(8,128)} %fusion.49, bf16[2048,3200]{1,0:T(8,128)(2,1)} %convolution_convert_fusion.1), kind=kLoop, calls=%fused_computation.10 | loop fusion | flops 78643200 | bytes 78643200
  368.7 23.0 %fusion.24 = bf16[2048,1024]{0,1:T(8,128)(2,1)} fusion(bf16[2048,3200]{1,0:T(8,128)(2,1)} %convolution_convert_fusion.1, f32[2048,3200]{1,0:T(8,128)} %fusion.54, bf16[1,1024,3200]{2,1,0:T(8,128)(2,1)} %all-gather.40.cloned.1.call-done), kind=kOutput, calls=%fused_computation.33 | convolution fusion | flops 13461094400 | bytes 50069504 | tf_op jit(solution)/vmap(transpose(jvp()))/dot_general | solution.py:21
  391.7 19.7 %fusion.43 = (f32[2048]{0:T(1024)S(1)}, bf16[2048,1024]{0,1:T(8,128)(2,1)S(1)}) fusion(bf16[1,2048,1024]{1,2,0:T(8,128)(2,1)S(1)} %copy-done.3, bf16[2048,1024]{0,1:T(8,128)(2,1)} %fusion.24, bf16[2048,3200]{1,0:T(8,128)(2,1)} %fusion.6, bf16[1,1024,3200]{2,1,0:T(8,128)(2,1)} %all-gather.36.cloned.1.call-done), kind=kOutput, calls=%fused_computation.62 | convolution fusion | flops 13432256512 | bytes 32251904 | tf_op jit(solution)/vmap(transpose(jvp()))/dot_general | solution.py:20
  416.2 23.1 %convolution_convert_fusion = bf16[2048,3200]{1,0:T(8,128)(2,1)} fusion(bf16[1,2048,1024]{1,2,0:T(8,128)(2,1)} %fusion.66, bf16[1,3200,1024]{2,0,1:T(2,128)(2,1)} %all-gather.34.cloned.1.call-done), kind=kOutput, calls=%fused_computation.34 | convolution fusion | flops 13428326400 | bytes 23855104 | tf_op jit(solution)/vmap(transpose(jvp()))/dot_general | solution.py:9
  439.3 26.0 %fusion.18 = f32[3200,1024]{0,1:T(8,128)} fusion(bf16[2048,3200]{1,0:T(8,128)(2,1)} %convolution_convert_fusion, f32[2048,3200]{1,0:T(8,128)} %fusion.61, bf16[1,2048,1024]{1,2,0:T(8,128)(2,1)} %copy.13, f32[2048]{0:T(1024)S(1)} %bitcast.245), kind=kOutput, calls=%fused_computation.30 | convolution fusion | flops 13467385856 | bytes 56631296 | tf_op jit(solution)/vmap(transpose(jvp()))/dot_general | solution.py:21
  465.5 22.1 %fusion.84 = f32[3200,1024]{0,1:T(8,128)} fusion(bf16[2048,3200]{1,0:T(8,128)(2,1)} %fusion.6, bf16[1,2048,1024]{1,2,0:T(8,128)(2,1)} %get-tuple-element.19, f32[2048]{0:T(1024)S(1)} %bitcast.252), kind=kOutput, calls=%fused_computation.95 | convolution fusion | flops 13428064256 | bytes 30416896 | tf_op jit(solution)/vmap(transpose(jvp()))/dot_general | solution.py:20
  487.7 28.7 %fusion.28 = f32[3200,1024]{1,0:T(8,128)} fusion(f32[2048,3200]{1,0:T(8,128)} %fusion.49, f32[2048,3200]{1,0:T(8,128)} %fusion.54, bf16[1,2048,1024]{2,1,0:T(8,128)(2,1)} %param), kind=kOutput, calls=%fused_computation.46 | convolution fusion | flops 13461094400 | bytes 69730304 | tf_op jit(solution)/vmap(transpose(jvp()))/dot_general | solution.py:9
  516.4 113.4 %fusion = f32[104,1024]{1,0:T(8,128)S(1)} fusion(f32[3200,1024]{1,0:T(8,128)} %fusion.28), kind=kCustom, calls=%all-reduce-scatter | all-reduce-scatter fusion | flops 3407873 | bytes 13533184
  629.8 26.9 %fusion.9 = bf16[2048,3200]{1,0:T(8,128)(2,1)} fusion(f32[2048,3200]{1,0:T(8,128)} %fusion.61, f32[2048,3200]{1,0:T(8,128)} %fusion.57, bf16[2048,3200]{1,0:T(8,128)(2,1)} %convolution_convert_fusion), kind=kLoop, calls=%fused_computation.13 | loop fusion | flops 78643200 | bytes 78643200
  656.8 22.0 %fusion.79 = f32[3200,1024]{0,1:T(8,128)} fusion(bf16[2048,3200]{1,0:T(8,128)(2,1)} %fusion.9, bf16[1,2048,1024]{1,2,0:T(8,128)(2,1)} %copy.13, f32[2048]{0:T(1024)S(1)} %bitcast.246), kind=kOutput, calls=%fused_computation.94 | convolution fusion | flops 13428064256 | bytes 30416896 | tf_op jit(solution)/vmap(transpose(jvp()))/dot_general | solution.py:20
  678.8 20.8 %fusion.67 = f32[1024,3200]{0,1:T(8,128)} fusion(bf16[2048,3200]{1,0:T(8,128)(2,1)} %fusion.26, bf16[1,2048,1024]{1,2,0:T(8,128)(2,1)} %fusion.66), kind=kOutput, calls=%fused_computation.86 | convolution fusion | flops 13421772800 | bytes 30408704 | tf_op jit(solution)/vmap(transpose(jvp()))/dot_general | solution.py:9
  699.7 97.8 %fusion.1 = f32[1024,104]{0,1:T(8,128)S(1)} fusion(f32[1024,3200]{0,1:T(8,128)} %fusion.67), kind=kCustom, calls=%all-reduce-scatter.1 | all-reduce-scatter fusion | flops 3407873 | bytes 13533184
  804.3 22.5 %fusion.20 = bf16[2048,1024]{0,1:T(8,128)(2,1)} fusion(bf16[2048,3200]{1,0:T(8,128)(2,1)} %convolution_convert_fusion, f32[2048,3200]{1,0:T(8,128)} %fusion.61, bf16[1,1024,3200]{2,1,0:T(8,128)(2,1)} %all-gather.32.cloned.1.call-done), kind=kOutput, calls=%fused_computation.31 | convolution fusion | flops 13461094400 | bytes 50069504 | tf_op jit(solution)/vmap(transpose(jvp()))/dot_general | solution.py:21
  826.8 19.7 %fusion.40 = (f32[2048]{0:T(1024)S(1)}, bf16[2048,1024]{0,1:T(8,128)(2,1)S(1)}) fusion(bf16[1,2048,1024]{1,2,0:T(8,128)(2,1)S(1)} %copy-done, bf16[2048,1024]{0,1:T(8,128)(2,1)} %fusion.20, bf16[2048,3200]{1,0:T(8,128)(2,1)} %fusion.9, bf16[1,1024,3200]{2,1,0:T(8,128)(2,1)} %all-gather.30.cloned.1.call-done), kind=kOutput, calls=%fused_computation.59 | convolution fusion | flops 13432256512 | bytes 32251904 | tf_op jit(solution)/vmap(transpose(jvp()))/dot_general | solution.py:20
  846.6 4.7 fusion.65
  851.3 6.4 copy.15
  864.0 22.6 %reduce-scatter.21.cloned.1.call-done = f32[3200,32]{0,1:T(8,128)} async-done(((f32[3200,1024]{0,1:T(8,128)}), f32[3200,32]{0,1:T(8,128)}) %reduce-scatter.21.cloned.1.call-update) | async-done | bytes 409616
  (83 shorter events, 33.0 us)
Async XLA Ops:
  7.2 51.4 %all-gather.30.cloned.1.call-start = ((), (), s32[]{:S(2)}) async-start(), calls=%async_computation.4 | async-start | bytes 6758400 | tf_op jit(solution)/vmap(jvp())/squeeze | solution.py:27
  9.1 94.6 %all-gather.32.cloned.1.call-start = ((), (), s32[]{:S(2)}) async-start(), calls=%async_computation.5 | async-start | bytes 6758400 | tf_op jit(solution)/vmap(jvp())/squeeze | solution.py:27
  11.1 152.7 %all-gather.34.cloned.1.call-start = ((), (), s32[]{:S(2)}) async-start(), calls=%async_computation.6 | async-start | bytes 13516800 | tf_op jit(solution)/vmap(jvp())/squeeze | solution.py:27
  13.9 210.4 %all-gather.38.cloned.1.call-start = ((), (), s32[]{:S(2)}) async-start(), calls=%async_computation.8 | async-start | bytes 13516800 | tf_op jit(solution)/vmap(jvp())/squeeze | solution.py:27
  14.6 255.4 %all-gather.36.cloned.1.call-start = ((), (), s32[]{:S(2)}) async-start(), calls=%async_computation.7 | async-start | bytes 6758400 | tf_op jit(solution)/vmap(jvp())/squeeze | solution.py:27
  15.2 303.4 %all-gather.40.cloned.1.call-start = ((), (), s32[]{:S(2)}) async-start(), calls=%async_computation.9 | async-start | bytes 6758400 | tf_op jit(solution)/vmap(jvp())/squeeze | solution.py:27
  15.9 844.3 %reduce-scatter.23.cloned.1.call-start = ((), (), s32[]{:S(2)}) async-start(), calls=%async_computation.12 | async-start | bytes 13516800
  25.5 0.6 copy-start.6
  26.1 77.6 %copy-start.10 = (f32[1,2048]{1,0:T(1,128)}, f32[1,2048]{1,0:T(1,128)S(1)}, u32[]{:S(2)}) copy-start(f32[1,2048]{1,0:T(1,128)S(1)} %rsqrt.22) | copy-start | bytes 24580
  186.5 0.6 copy-start.8
  368.6 492.6 %reduce-scatter.25.cloned.1.call-start = ((), (), s32[]{:S(2)}) async-start(), calls=%async_computation.13 | async-start | bytes 13516800
  368.7 23.1 %copy-start.3 = (bf16[1,2048,1024]{1,2,0:T(8,128)(2,1)S(1)}, bf16[1,2048,1024]{1,2,0:T(8,128)(2,1)}, u32[]{:S(2)}) copy-start(bf16[1,2048,1024]{1,2,0:T(8,128)(2,1)} %get-tuple-element.19) | copy-start | bytes 12582916
  391.7 19.7 %copy-start.9 = (f32[2048]{0:T(1024)S(1)}, f32[2048]{0:T(1024)}, u32[]{:S(2)}) copy-start(f32[2048]{0:T(1024)} %copy-done.8) | copy-start | bytes 24580
  391.7 19.8 %copy-start.2 = (bf16[1,2048,1024]{1,2,0:T(8,128)(2,1)S(1)}, bf16[1,2048,1024]{1,2,0:T(8,128)(2,1)}, u32[]{:S(2)}) copy-start(bf16[1,2048,1024]{1,2,0:T(8,128)(2,1)} %copy.14) | copy-start | bytes 12582916
  416.2 23.1 %copy-start.11 = (f32[1,2048]{1,0:T(1,128)S(1)}, f32[1,2048]{1,0:T(1,128)}, u32[]{:S(2)}) copy-start(f32[1,2048]{1,0:T(1,128)} %copy-done.10) | copy-start | bytes 24580
  465.4 397.6 %reduce-scatter.19.cloned.1.call-start = ((), (), s32[]{:S(2)}) async-start(), calls=%async_computation.10 | async-start | bytes 13516800
  487.6 399.0 %reduce-scatter.21.cloned.1.call-start = ((), (), s32[]{:S(2)}) async-start(), calls=%async_computation.11 | async-start | bytes 13516800
  629.7 27.0 %copy-start.4 = (f32[104,1024]{1,0:T(8,128)}, f32[104,1024]{1,0:T(8,128)S(1)}, u32[]{:S(2)}) copy-start(f32[104,1024]{1,0:T(8,128)S(1)} %fusion) | copy-start | bytes 1277956
  797.5 29.3 %copy-start = (bf16[1,2048,1024]{1,2,0:T(8,128)(2,1)S(1)}, bf16[1,2048,1024]{1,2,0:T(8,128)(2,1)}, u32[]{:S(2)}) copy-start(bf16[1,2048,1024]{1,2,0:T(8,128)(2,1)} %copy.13) | copy-start | bytes 12582916
  797.5 60.2 %collective-permute-start = (bf16[104,1024]{1,0:T(8,128)(2,1)S(1)}, bf16[104,1024]{1,0:T(8,128)(2,1)S(1)}, u32[]{:S(2)}, u32[]{:S(2)}) collective-permute-start(bf16[104,1024]{1,0:T(8,128)(2,1)S(1)} %convert.43), channel_id=1, source_target_pairs={{0,1},{1,2},{2,3},{3,4},{4,5},{5,6},{6,7},{7,8},{8,9},{9,10},{10,1... | collective-permute-start | bytes 638984
  799.7 58.0 %collective-permute-start.1 = (bf16[20,1024]{1,0:T(8,128)(2,1)S(1)}, bf16[20,1024]{1,0:T(8,128)(2,1)S(1)}, u32[]{:S(2)}, u32[]{:S(2)}) collective-permute-start(bf16[20,1024]{1,0:T(8,128)(2,1)S(1)} %slice.24), channel_id=1, source_target_pairs={{0,2},{1,3},{2,4},{3,5},{4,6},{5,7},{6,8},{7,9},{8,10},{9,11},{10,... | collective-permute-start | bytes 122888
  801.1 57.2 %collective-permute-start.2 = (bf16[1024,104]{0,1:T(8,128)(2,1)S(1)}, bf16[1024,104]{0,1:T(8,128)(2,1)S(1)}, u32[]{:S(2)}, u32[]{:S(2)}) collective-permute-start(bf16[1024,104]{0,1:T(8,128)(2,1)S(1)} %convert.42), channel_id=1, source_target_pairs={{0,1},{1,2},{2,3},{3,4},{4,5},{5,6},{6,7},{7,8},{8,9},{9,10},{10,1... | collective-permute-start | bytes 638984
  803.0 55.2 %collective-permute-start.3 = (bf16[1024,20]{0,1:T(8,128)(2,1)S(1)}, bf16[1024,20]{0,1:T(8,128)(2,1)S(1)}, u32[]{:S(2)}, u32[]{:S(2)}) collective-permute-start(bf16[1024,20]{0,1:T(8,128)(2,1)S(1)} %slice.25), channel_id=1, source_target_pairs={{0,2},{1,3},{2,4},{3,5},{4,6},{5,7},{6,8},{7,9},{8,10},{9,11},{10,... | collective-permute-start | bytes 122888
  826.8 19.8 %copy-start.7 = (f32[2048]{0:T(1024)S(1)}, f32[2048]{0:T(1024)}, u32[]{:S(2)}) copy-start(f32[2048]{0:T(1024)} %copy-done.6) | copy-start | bytes 24580
  826.8 19.8 %copy-start.1 = (bf16[1,2048,1024]{1,2,0:T(8,128)(2,1)S(1)}, bf16[1,2048,1024]{1,2,0:T(8,128)(2,1)}, u32[]{:S(2)}) copy-start(bf16[1,2048,1024]{1,2,0:T(8,128)(2,1)} %fusion.66) | copy-start | bytes 12582916
  846.5 11.2 %copy-start.5 = (f32[104,1024]{1,0:T(8,128)S(1)}, f32[104,1024]{1,0:T(8,128)}, u32[]{:S(2)}) copy-start(f32[104,1024]{1,0:T(8,128)} %copy-done.4) | copy-start | bytes 1277956
Sparse Core Ops, SparseCore 0:
  10.1 48.4 all-gather.29
  60.7 42.9 all-gather.31
  106.4 57.3 all-gather.33
  166.2 58.0 all-gather.37
  226.3 43.6 all-gather.35
  272.5 42.9 all-gather.39
  368.7 94.3 reduce-scatter.22
  466.8 138.2 reduce-scatter.24
  608.8 148.5 reduce-scatter.18
  760.9 125.6 reduce-scatter.20
where the time goes:
time: 905 us; the launch traced here: 896 us
  matrix products  391 us (43%)
  blocking collectives  211 us (23%)
  waiting for transfers between devices  147 us (16%)
  other arithmetic  95 us (10%)
  local copies, waits for them, and re-layouts  29.3 us (3%)
  between operations  14.9 us (2%)
    unnamed x2, blocking collectives  211 us
    dot_general x6, matrix products, layer(): up = jnp.dot(a, w['w_up'], preferred_element_type=jnp.float32)  143 us
    dot_general x6, matrix products, layer(): gate = jnp.dot(a, w['w_gate'], preferred_element_type=jnp.float32)  130 us
    squeeze x6, waiting for transfers between devices, stack(): h = layer(h, {name: w[number] for name, w in weights.items()})  122 us
    dot_general x5, matrix products, matmul(): jnp.dot(a, w, preferred_element_type=jnp.float32).astype(jnp.bfloat16)  118 us
    unnamed x5, other arithmetic  76.8 us
    unnamed x18, waiting for transfers between devices  24.7 us
    unnamed x32, local copies, waits for them, and re-layouts  22.8 us
  transfers between devices with their start and end apart: 14, of which 6 were waited for; matrix products, arithmetic and copies ran while one was open for 75% of the time, Pallas kernels for 0%

commit v1 on v0

v1 whole, which is shorter than its diff:
```python
import functools
import math

import jax
import jax.numpy as jnp
from jax import lax
from jax.experimental import pallas as pl
from jax.experimental.pallas import tpu as pltpu
from jax.sharding import PartitionSpec as P

F32, BF16 = jnp.float32, jnp.bfloat16
MESH = pl.DeviceIdType.MESH
ALL = slice(None)
RING = 4
EPS = 1e-6
BM = 256
VMEM_LIMIT = 66_000_000


class Place:
    def __init__(self):
        me = lax.axis_index("dp")
        self.core = lax.rem(me, 2)
        chip = me // 2
        self.y = lax.rem(chip, RING)
        self.x = chip // RING

    def device(self, colour, p, q, core=None):
        x, y = (p, q) if colour == 0 else (q, p)
        return {"dp": (x * RING + y) * 2 + (self.core if core is None else core)}

    def peer(self):
        return self.device(0, self.x, self.y, 1 - self.core)

    def pq(self, colour):
        return (self.x, self.y) if colour == 0 else (self.y, self.x)


def ahead(i, by):
    return lax.rem(i + by, RING)


def greet():
    here = Place()
    barrier = pltpu.get_barrier_semaphore()
    (x, y) = here.x, here.y
    others = [here.peer()]
    for by in (1, RING - 1):
        others += [here.device(0, ahead(x, by), y), here.device(0, x, ahead(y, by))]
    for other in others:
        pl.semaphore_signal(barrier, inc=1, device_id=other, device_id_type=MESH)
    pl.semaphore_wait(barrier, len(others))


class Piece:
    def __init__(self, kind, rows, columns):
        self.kind, self.rows, self.columns = kind, rows, columns

    def sub(self, colour, half):
        if self.kind == "row":
            r = (self.rows // 2 * colour, self.rows // 2)
            first = (self.columns // 128 + 1) // 2 * 128
            c = {None: (0, self.columns), 0: (0, first), 1: (first, self.columns - first)}[half]
        else:
            r = (0, self.rows)
            wide = self.columns // 2
            c = {None: (0, wide), 0: (0, wide // 2), 1: (wide // 2, wide // 2)}[half]
            c = (c[0] + wide * colour, c[1])
        return r, c

    def shape(self, colour, half):
        r, c = self.sub(colour, half)
        return (r[1], c[1])

    def inside(self, half):
        r, c = self.sub(0, half)
        return pl.ds(c[0], c[1])

    def of_whole(self, ref, core, colour, p, q, half=None):
        x, y = (p, q) if colour == 0 else (q, p)
        r, c = self.sub(colour, half)
        if self.kind == "row":
            return ref.at[x, y, core, pl.ds(*r), pl.ds(*c)]
        return ref.at[x, y, pl.ds(*r), pl.ds(pl.multiple_of(core * self.columns + c[0], 128), c[1])]

    def all_of_core(self, ref, core):
        if self.kind == "row":
            return ref.at[:, :, core]
        return ref.at[:, :, :, pl.ds(pl.multiple_of(core * self.columns, 128), self.columns)]

    def chip_of_core(self, ref, core, x, y):
        if self.kind == "row":
            return ref.at[x, y, core]
        return ref.at[x, y, :, pl.ds(pl.multiple_of(core * self.columns, 128), self.columns)]

    def of_own(self, ref, colour, half=None):
        r, c = self.sub(colour, half)
        return ref.at[pl.ds(*r), pl.ds(*c)]

    def of_pieces(self, ref, colour, p, q, half=None):
        x, y = (p, q) if colour == 0 else (q, p)
        r, c = self.sub(colour, half)
        return ref.at[x, y, pl.ds(*r), pl.ds(*c)]

    def whole_shape(self):
        if self.kind == "row":
            return (RING, RING, 2, self.rows, self.columns)
        return (RING, RING, self.rows, 2 * self.columns)


def remote(src, dst, sems, k, device):
    send, recv = sems
    return pltpu.make_async_remote_copy(
        src_ref=src, dst_ref=dst, send_sem=send.at[k], recv_sem=recv.at[k], device_id=device, device_id_type=MESH
    )


class Gather:
    N = 24

    def __init__(self, piece):
        self.piece = piece

    def scratch(self):
        return [pltpu.SemaphoreType.DMA((self.N,)), pltpu.SemaphoreType.DMA((self.N,)), pltpu.SemaphoreType.DMA]

    def bind(self, own, whole, send, recv, local):
        self.own, self.whole, self.sems, self.local = own, whole, (send, recv), local
        return self

    def copies(self, here):
        piece, own, whole, core = self.piece, self.own, self.whole, here.core
        out = {}

        def of_colour(colour):
            p, q = here.pq(colour)
            p1, pm, q1, qm = ahead(p, 1), ahead(p, RING - 1), ahead(q, 1), ahead(q, RING - 1)
            q2 = ahead(q, 2)
            at = functools.partial(piece.of_whole, whole, core, colour)
            dev = functools.partial(here.device, colour)
            base = 12 * colour

            def add(name, k, src, dst, device):
                out[name, colour] = lambda: remote(src(), dst(), self.sems, base + k, device)

            mine = lambda: piece.of_own(own, colour)
            add("s1+", 0, mine, lambda: at(p, q), dev(p1, q))
            add("s1-", 1, mine, lambda: at(p, q), dev(pm, q))
            add("s2+", 2, lambda: at(pm, q, 0), lambda: at(pm, q, 0), dev(p1, q))
            add("s2-", 3, lambda: at(p1, q, 1), lambda: at(p1, q, 1), dev(pm, q))
            add("s3+", 4, lambda: at(ALL, q), lambda: at(ALL, q), dev(p, q1))
            add("s3-", 5, lambda: at(ALL, q), lambda: at(ALL, q), dev(p, qm))
            add("s4+", 6, lambda: at(ALL, qm, 0), lambda: at(ALL, qm, 0), dev(p, q1))
            add("s4-", 7, lambda: at(ALL, q1, 1), lambda: at(ALL, q1, 1), dev(p, qm))
            for k, of in ((8, q), (9, qm), (10, q1), (11, q2)):
                add(f"d{k}", k, lambda of=of: at(ALL, of), lambda of=of: at(ALL, of), here.peer())

        of_colour(0)
        of_colour(1)
        return out

    def run(self, stage):
        here = Place()
        c = self.copies(here)
        both = lambda names, do: [do(c[name, colour]()) for name in names for colour in (0, 1)]
        start = lambda *names: both(names, lambda d: d.start())
        arrived = lambda *names: both(names, lambda d: d.wait_recv())
        local = lambda: pltpu.make_async_copy(
            self.own, self.piece.chip_of_core(self.whole, here.core, here.x, here.y), self.local
        )
        if stage == 0:
            start("s1+", "s1-")
            local().start()
        elif stage == 1:
            for name, then in (("s1+", "s2+"), ("s1-", "s2-")):
                arrived(name)
                start(then)
        elif stage == 2:
            local().wait()
            arrived("s2+", "s2-")
            start("s3+", "s3-", "d8")
        elif stage == 3:
            for name, then, peer in (("s3+", "s4+", "d9"), ("s3-", "s4-", "d10")):
                arrived(name)
                start(then, peer)
        elif stage == 4:
            arrived("s4+", "s4-")
            start("d11")
        else:
            arrived("d8", "d9", "d10", "d11")
            both([n for n, colour in c if colour == 0], lambda d: d.wait_send())

    STAGES = 6


class Scatter:
    STAGES = 6

    def __init__(self, piece):
        self.piece = piece

    def scratch(self):
        piece = self.piece
        full = (RING, RING, piece.rows, piece.columns)
        c, h0, h1 = piece.shape(0, None), piece.shape(0, 0), piece.shape(0, 1)
        vm = lambda *shape, dtype=BF16: pltpu.VMEM(shape, dtype)
        per = [
            vm(2, RING, *h0), vm(2, RING, *h1), vm(2, RING, *c), vm(2, RING, *c),
            vm(2, *h0), vm(2, *h1), vm(2, *c), vm(2, *c),
            vm(2, RING, *c, dtype=F32),
        ]
        return [
            vm(*full), vm(*full), *per,
            pltpu.SemaphoreType.DMA((17,)), pltpu.SemaphoreType.DMA((17,)), pltpu.SemaphoreType.DMA,
        ]

    def bind(self, terms, result, *scratch):
        self.terms, self.result = terms, result
        self.t, self.r, *self.landing, self.acc, send, recv, self.local = scratch
        self.sems = (send, recv)
        return self

    def copies(self, here):
        piece, t = self.piece, self.t
        far_a, far_b, near_a, near_b, last_far_a, last_far_b, last_near_a, last_near_b = self.landing
        out = {}

        def of_colour(colour):
            p, q = here.pq(colour)
            p1, pm, p2 = ahead(p, 1), ahead(p, RING - 1), ahead(p, 2)
            q1, qm, q2 = ahead(q, 1), ahead(q, RING - 1), ahead(q, 2)
            at = functools.partial(piece.of_pieces, t, colour)
            dev = functools.partial(here.device, colour)
            base = 8 * colour

            def add(name, k, src, dst, device):
                out[name, colour] = lambda: remote(src(), dst.at[colour], self.sems, base + k, device)

            add("F+", 0, lambda: at(ALL, q2, 0), far_a, dev(p, q1))
            add("F-", 1, lambda: at(ALL, q2, 1), far_b, dev(p, qm))
            add("N+", 2, lambda: at(ALL, q1), near_a, dev(p, q1))
            add("N-", 3, lambda: at(ALL, qm), near_b, dev(p, qm))
            add("f+", 4, lambda: at(p2, q, 0), last_far_a, dev(p1, q))
            add("f-", 5, lambda: at(p2, q, 1), last_far_b, dev(pm, q))
            add("n+", 6, lambda: at(p1, q), last_near_a, dev(p1, q))
            add("n-", 7, lambda: at(pm, q), last_near_b, dev(pm, q))

        of_colour(0)
        of_colour(1)
        return out

    def run(self, stage):
        here = Place()
        piece, t, r, acc = self.piece, self.t, self.r, self.acc
        far_a, far_b, near_a, near_b, last_far_a, last_far_b, last_near_a, last_near_b = self.landing
        c = self.copies(here)
        both = lambda names, do: [do(c[name, colour]()) for name in names for colour in (0, 1)]
        arrived = lambda *names: both(names, lambda d: d.wait_recv())
        peer = lambda: remote(piece.all_of_core(self.terms, 1 - here.core), r, self.sems, 16, here.peer())
        local = lambda: pltpu.make_async_copy(piece.all_of_core(self.terms, here.core), t, self.local)
        wide = lambda ref: ref[...].astype(F32)
        if stage == 0:
            peer().start()
            local().start()
            return
        if stage == 1:
            local().wait()
            peer().wait_recv()
        if stage == 2:
            arrived("F+", "F-")
        if stage == 3:
            arrived("N+", "N-")
        if stage == 4:
            arrived("f+", "f-")
        if stage == 5:
            arrived("n+", "n-")
        for colour in (0, 1):
            p, q = here.pq(colour)
            p1, pm, p2 = ahead(p, 1), ahead(p, RING - 1), ahead(p, 2)
            q1, qm, q2 = ahead(q, 1), ahead(q, RING - 1), ahead(q, 2)
            own = lambda pp, qq, half=None: wide(piece.of_pieces(t, colour, pp, qq, half)) + wide(
                piece.of_pieces(r, colour, pp, qq, half)
            )

            def put(pp, qq, value, half=None):
                piece.of_pieces(t, colour, pp, qq, half)[...] = value.astype(BF16)

            h0, h1 = piece.inside(0), piece.inside(1)
            if stage == 1:
                for i in range(RING):
                    put(i, q2, own(i, q2))
                c["F+", colour]().start()
                c["F-", colour]().start()
            elif stage == 2:
                for i in range(RING):
                    put(i, q1, own(i, q1, 0) + far_a[colour, i].astype(F32), 0)
                    put(i, q1, own(i, q1, 1), 1)
                c["N+", colour]().start()
                for i in range(RING):
                    put(i, qm, own(i, qm, 0), 0)
                    put(i, qm, own(i, qm, 1) + far_b[colour, i].astype(F32), 1)
                c["N-", colour]().start()
            elif stage == 3:
                for i in range(RING):
                    acc[colour, i] = own(i, q) + near_a[colour, i].astype(F32) + near_b[colour, i].astype(F32)
                put(p2, q, acc[colour, p2])
                c["f+", colour]().start()
                c["f-", colour]().start()
            elif stage == 4:
                put(p1, q, acc[colour, p1, :, h0] + last_far_a[colour].astype(F32), 0)
                put(p1, q, acc[colour, p1, :, h1], 1)
                c["n+", colour]().start()
                put(pm, q, acc[colour, pm, :, h0], 0)
                put(pm, q, acc[colour, pm, :, h1] + last_far_b[colour].astype(F32), 1)
                c["n-", colour]().start()
            else:
                total = acc[colour, p] + last_near_a[colour].astype(F32) + last_near_b[colour].astype(F32)
                piece.of_own(self.result, colour)[...] = total.astype(BF16)
        if stage == 5:
            peer().wait_send()
            both([n for n, colour in c if colour == 0], lambda d: d.wait_send())


def kernel_call(name, grid, compute, inputs, outputs, parts=1, gathers=(), scatters=(), at=None, collective_id=None, scratch=()):
    comms = [Gather(p) for p, _ in gathers] + [Scatter(p) for p, _ in scatters]
    n_in, n_out = len(inputs), len(outputs)
    steps = math.prod(grid)
    any_space = pl.BlockSpec(memory_space=pltpu.HBM)
    in_vmem = lambda shape: pl.BlockSpec(shape, lambda *_: (0,) * len(shape), pipeline_mode=pl.Buffered(1))

    def spec(block, index):
        if index is None:
            return in_vmem(block)
        return pl.BlockSpec(block, index)

    in_specs = [spec(b, i) for _, b, i in inputs]
    out_specs = [spec(b, i) for *_, b, i in outputs]
    out_shape = [jax.ShapeDtypeStruct(s, d) for s, d, *_ in outputs]
    args = [a for a, *_ in inputs]
    for piece, own in gathers:
        args.append(own)
        in_specs.append(in_vmem(own.shape))
        out_shape.append(jax.ShapeDtypeStruct(piece.whole_shape(), BF16))
        out_specs.append(any_space)
    for piece, terms in scatters:
        args.append(terms)
        in_specs.append(any_space)
        shape = (piece.rows, piece.columns)
        out_shape.append(jax.ShapeDtypeStruct(shape, BF16))
        out_specs.append(in_vmem(shape))
    comm_scratch = [c.scratch() for c in comms]
    scratch_shapes = [*scratch, *(s for group in comm_scratch for s in group)]
    last = steps * parts
    if comms and at is None:
        at = [min(last, k * last // 6) for k in range(6)]

    def body(*refs):
        refs = list(refs)
        take = lambda n: [refs.pop(0) for _ in range(n)]
        ins, comm_in = take(n_in), take(len(comms))
        outs, comm_out = take(n_out), take(len(comms))
        own_scratch = take(len(scratch))
        for comm, i, o, s in zip(comms, comm_in, comm_out, comm_scratch):
            comm.bind(i, o, *take(len(s)))
        step = pl.program_id(0)
        for d in range(1, len(grid)):
            step = step * grid[d] + pl.program_id(d)

        def act(slot):
            if slot == 0:
                greet()
            for k in range(6):
                if at[k] == slot:
                    for comm in comms:
                        comm.run(k)

        def hook(part):
            if not comms:
                return
            for slot in sorted({0, *at}):
                if slot < last and slot % parts == part:
                    pl.when(step == slot // parts)(functools.partial(act, slot))

        compute(hook, step, ins, outs, own_scratch)
        if comms and any(a == last for a in at):
            pl.when(step == steps - 1)(functools.partial(act, last))

    params = dict(vmem_limit_bytes=VMEM_LIMIT, dimension_semantics=("arbitrary",) * len(grid))
    if comms:
        params |= dict(collective_id=collective_id, has_side_effects=True)
    return pl.pallas_call(
        body, grid=grid, in_specs=in_specs, out_specs=out_specs, out_shape=out_shape, scratch_shapes=scratch_shapes,
        compiler_params=pltpu.CompilerParams(**params), name=name,
    )(*args)


def dot(a, b, ca=1, cb=0):
    return lax.dot_general(a, b, (((ca,), (cb,)), ((), ())), preferred_element_type=F32)


def chunks(n, size=512):
    return [(i, min(size, n - i)) for i in range(0, n, size)]


def normed(h):
    wide = h.astype(F32)
    scale = lax.rsqrt(jnp.mean(wide**2, -1, keepdims=True) + EPS)
    return (wide * scale).astype(BF16)


def norm_back(h, da, dy):
    wide, da = h.astype(F32), da.astype(F32)
    scale = lax.rsqrt(jnp.mean(wide**2, -1, keepdims=True) + EPS)
    by_scale = jnp.sum(da * wide, -1, keepdims=True)
    by_mean = by_scale * (-0.5) * scale * scale * scale
    return dy + (da * scale + wide * (by_mean * (2.0 / h.shape[-1]))).astype(BF16)


def gated(g, u):
    s = jax.nn.sigmoid(g)
    return (g * s * u).astype(BF16)


def gated_back(g, u, dh):
    s = jax.nn.sigmoid(g)
    silu = g * s
    return ((dh * u) * (s + silu * (1.0 - s))).astype(BF16), (dh * silu).astype(BF16)


def rows_of(array, bm=BM):
    block = (bm, *array.shape[1:])
    return array, block, lambda i: (i, 0)


def whole(array):
    return array, array.shape, None


def k_norm(x, **comm):
    t, d = x.shape

    def compute(hook, step, ins, outs, _):
        hook(0)
        outs[0][...] = normed(ins[0][...])

    bm = t // 8
    return kernel_call("norm", (8,), compute, [rows_of(x, bm)], [((t, d), BF16, (bm, d), lambda i: (i, 0))], **comm)


def k_gate_up(a, wg, wu, **comm):
    t, f = a.shape[0], wg.shape[1]

    def compute(hook, step, ins, outs, _):
        a, wg, wu = ins
        g_out, u_out, h_out = outs
        x = a[...]
        hook(0)
        for lo, n in chunks(f):
            cols = pl.ds(lo, n)
            g, u = dot(x, wg[:, cols]), dot(x, wu[:, cols])
            g_out[:, cols] = g
            u_out[:, cols] = u
            h_out[:, cols] = gated(g, u)

    o = lambda dt: ((t, f), dt, (BM, f), lambda i: (i, 0))
    return kernel_call("gate_up", (t // BM,), compute, [rows_of(a), whole(wg), whole(wu)], [o(F32), o(F32), o(BF16)], **comm)


def k_down(h, x, wd, **comm):
    t, d = x.shape

    def compute(hook, step, ins, outs, _):
        h, x, wd = ins
        hook(0)
        y = x[...] + dot(h[...], wd[...]).astype(BF16)
        outs[0][...] = y
        outs[1][...] = normed(y)

    o = ((t, d), BF16, (BM, d), lambda i: (i, 0))
    return kernel_call("down", (t // BM,), compute, [rows_of(h), rows_of(x), whole(wd)], [o, o], **comm)


def k_middle(a, dy, wg, wu, wd):
    t, f = a.shape[0], wg.shape[1]

    def compute(hook, step, ins, outs, _):
        a, dy, wg, wu, wd = ins
        dgu, h_out = outs
        x, dy = a[...], dy[...]
        for lo, n in chunks(f):
            cols = pl.ds(lo, n)
            g, u = dot(x, wg[:, cols]), dot(x, wu[:, cols])
            dh = dot(dy, wd[cols, :], 1, 1).astype(BF16).astype(F32)
            h_out[:, cols] = gated(g, u)
            dgu[0, :, cols], dgu[1, :, cols] = gated_back(g, u, dh)

    return kernel_call(
        "middle", (t // BM,), compute,
        [rows_of(a), rows_of(dy), whole(wg), whole(wu), whole(wd)],
        [((2, t, f), BF16, (2, BM, f), lambda i: (0, i, 0)), ((t, f), BF16, (BM, f), lambda i: (i, 0))],
    )


def k_hidden_back(dy, g, u, wd, **comm):
    t, f = g.shape

    def compute(hook, step, ins, outs, _):
        dy, g, u, wd = ins
        (dgu,) = outs
        hook(0)
        x = dy[...]
        for lo, n in chunks(f):
            cols = pl.ds(lo, n)
            dh = dot(x, wd[cols, :], 1, 1).astype(BF16).astype(F32)
            dgu[0, :, cols], dgu[1, :, cols] = gated_back(g[:, cols], u[:, cols], dh)

    return kernel_call(
        "hidden_back", (t // BM,), compute, [rows_of(dy), rows_of(g), rows_of(u), whole(wd)],
        [((2, t, f), BF16, (2, BM, f), lambda i: (0, i, 0))], **comm,
    )


def k_grad_down(h, dy, **comm):
    (t, f), d = h.shape, dy.shape[1]
    bn = f // 5

    def compute(hook, step, ins, outs, _):
        hook(0)
        outs[0][...] = dot(ins[0][...], ins[1][...], 0, 0).astype(BF16)

    return kernel_call(
        "grad_down", (5,), compute, [(h, (t, bn), lambda i: (0, i)), whole(dy)],
        [((f, d), BF16, (bn, d), lambda i: (i, 0))], **comm,
    )


def k_grad_gate_up(a, dgu, **comm):
    (t, d), f = a.shape, dgu.shape[2]
    bm = d // 4

    def compute(hook, step, ins, outs, _):
        a, dgu = ins
        x = a[...]
        hook(0)
        for lo, n in chunks(f):
            cols = pl.ds(lo, n)
            outs[0][0, :, cols] = dot(x, dgu[0, :, cols], 0, 0).astype(BF16)

    return kernel_call(
        "grad_gate_up", (2, 4), compute,
        [(a, (t, bm), lambda w, i: (0, i)), (dgu, (1, t, f), lambda w, i: (w, 0, 0))],
        [((2, d, f), BF16, (1, bm, f), lambda w, i: (w, i, 0))], **comm,
    )


def k_input_back(dgu, wg, wu, x, dy, **comm):
    t, d = x.shape
    f = dgu.shape[2]

    def compute(hook, step, ins, outs, _):
        dgu, wg, wu, x, dy = ins
        hook(0)
        da = dot(dgu[0], wg[...], 1, 1).astype(BF16) + dot(dgu[1], wu[...], 1, 1).astype(BF16)
        outs[0][...] = norm_back(x[...], da, dy[...])

    return kernel_call(
        "input_back", (t // BM,), compute,
        [(dgu, (2, BM, f), lambda i: (0, i, 0)), whole(wg), whole(wu), rows_of(x), rows_of(dy)],
        [((t, d), BF16, (BM, d), lambda i: (i, 0))], **comm,
    )


def solution(mesh):
    members = mesh.shape["dp"]
    swap = [(i, i ^ 1) for i in range(members)]

    def step(x, dy, w_gate, w_up, w_down):
        x, dy = x[0], dy[0]
        core = lax.rem(lax.axis_index("dp"), 2)
        rows, f = w_gate.shape[1:]
        deep, d = w_down.shape[1:]
        half = d // 2
        row, col = Piece("row", rows, f), Piece("col", 2 * deep, half)
        square = lambda w: w.reshape(-1, w.shape[-1])

        keep = lax.dynamic_slice_in_dim(w_down, core * half, half, 2)
        other = lax.ppermute(lax.dynamic_slice_in_dim(w_down, (1 - core) * half, half, 2), "dp", swap)
        down = jnp.where(core == 0, jnp.concatenate([keep, other], 1), jnp.concatenate([other, keep], 1))

        a0, wg0, wu0 = k_norm(x, gathers=[(row, w_gate[0]), (row, w_up[0])], collective_id=0)
        wg0, wu0 = square(wg0), square(wu0)
        g0, u0, h0, wd0, wg1 = k_gate_up(a0, wg0, wu0, gathers=[(col, down[0]), (row, w_gate[1])], collective_id=1)
        wd0, wg1 = square(wd0), square(wg1)
        x1, a1, wu1, wd1 = k_down(h0, x, wd0, gathers=[(row, w_up[1]), (col, down[1])], collective_id=2)
        wu1, wd1 = square(wu1), square(wd1)

        as_row = lambda g: g.reshape(RING, RING, 2, rows, f)
        as_col = lambda g: g.reshape(RING, RING, 2 * deep, d)
        dgu1, h1 = k_middle(a1, dy, wg1, wu1, wd1)
        (gd1,) = k_grad_down(h1, dy)
        ggu1, by_d1 = k_grad_gate_up(a1, dgu1, scatters=[(col, as_col(gd1))], collective_id=3)
        dx1, by_g1 = k_input_back(dgu1, wg1, wu1, x1, dy, scatters=[(row, as_row(ggu1[0]))], collective_id=4)
        dgu0, by_u1 = k_hidden_back(dx1, g0, u0, wd0, scatters=[(row, as_row(ggu1[1]))], collective_id=5)
        (gd0,) = k_grad_down(h0, dx1)
        ggu0, by_d0 = k_grad_gate_up(a0, dgu0, scatters=[(col, as_col(gd0))], collective_id=6)
        by_x, by_g0, by_u0 = k_input_back(
            dgu0, wg0, wu0, x, dx1, scatters=[(row, as_row(ggu0[0])), (row, as_row(ggu0[1]))], collective_id=7
        )

        by_down = jnp.stack([by_d0, by_d1])
        mine = lax.dynamic_slice_in_dim(by_down, core * deep, deep, 1)
        theirs = lax.ppermute(lax.dynamic_slice_in_dim(by_down, (1 - core) * deep, deep, 1), "dp", swap)
        by_down = jnp.where(core == 0, jnp.concatenate([mine, theirs], 2), jnp.concatenate([theirs, mine], 2))
        return by_x[None], jnp.stack([by_g0, by_g1]), jnp.stack([by_u0, by_u1]), by_down

    tokens, weights, grads = P(("rep", "dp")), P(None, "dp"), P("rep", "dp")
    return jax.shard_map(
        step, mesh=mesh, in_specs=(tokens, tokens, weights, weights, weights), out_specs=(tokens, grads, grads, grads),
        check_vma=False,
    )
```

time: 905 us -> 560 us (0.62)
  Pallas kernels: 0 us -> 513 us
  matrix products: 391 us -> 0 us
  blocking collectives: 211 us -> 0 us
  waiting for transfers between devices: 147 us -> 0.01 us
  other arithmetic: 95 us -> 3.93 us
  between operations: 14.9 us -> 1.01 us
    pallas_call x0 -> x11, Pallas kernels: none -> 513 us  [kernel_call(): pl.pallas_call(body, grid=grid, in_specs=in_specs, out_specs=out_specs, o...]
    dot_general x17 -> x0, matrix products: 391 us -> none  [the longest x6 143 us: layer(): up = jnp.dot(a, w['w_up'], preferred_element_type=jnp.float32)]
    unnamed x2 -> x0, blocking collectives: 211 us -> none
    squeeze x6 -> x0, waiting for transfers between devices: 122 us -> none  [stack(): h = layer(h, {name: w[number] for name, w in weights.items()})]
    unnamed x5 -> x0, other arithmetic: 76.8 us -> none
    unnamed x18 -> x0, waiting for transfers between devices: 24.7 us -> none
    unnamed x32 -> x10, local copies, waits for them, and re-layouts: 22.8 us -> 5.87 us
    slice x3 -> x2, local copies, waits for them, and re-layouts: 6.36 us -> 21.3 us  [the longest x1 10.7 us: step(): ggu0[1]]
  transfers between devices with their start and end apart: 14 -> 2, of which waited for: 6 -> 0; matrix products, arithmetic and copies ran while one was open for 75% -> 1% of each run, Pallas kernels for 0% -> 20%
where the time goes in v1:
time: 560 us; the launch traced here: 552 us
  Pallas kernels  513 us (92%)
  local copies, waits for them, and re-layouts  31.4 us (6%)
    pallas_call x11, Pallas kernels, kernel_call(): pl.pallas_call(body, grid=grid, in_specs=in_specs, out_specs=out_specs, o...  513 us
  transfers between devices with their start and end apart: 2, of which 0 were waited for; matrix products, arithmetic and copies ran while one was open for 1% of the time, Pallas kernels for 20%

profile of v1, /device:TPU:97, one launch (start us, length us, event | category | flops | bytes accessed | tf_op | source)
XLA Modules:
  0.0 552.3 jit_solution(5192647520371795449)
XLA Ops:
  0.6 1.3 constant_dynamic-slice_fusion.1
  2.0 2.1 collective-permute-start
  4.1 2.1 slice_bitcast_fusion.2
  6.3 47.8 %norm.1 = (bf16[2048,1024]{1,0:T(8,128)(2,1)}, bf16[4,4,2,32,3200]{4,3,2,1,0:T(8,128)(2,1)}, bf16[4,4,2,32,3200]{4,3,2,1,0:T(8,128)(2,1)}) custom-call(bf16[2048,1024]{1,0:T(8,128)(2,1)} %bitcast.36, bf16[32,3200]{1,0:T(8,128)(2,1)} %get-tuple-element.72.refs_1_, bf16[32,3200]{1,0:T(8,128)(2,1)} %get-tuple-element.67.refs_2_), custom_call_target="tpu_custom_call" | custom-call | tf_op jit(solution)/shard_map/norm/pallas_call | solution.py:391
  54.1 0.0 collective-permute-done
  54.1 0.1 maximum_select_fusion.1
  54.2 0.8 slice_bitcast_fusion
  55.0 59.8 %gate_up.1 = (f32[2048,3200]{1,0:T(8,128)}, f32[2048,3200]{1,0:T(8,128)}, bf16[2048,3200]{1,0:T(8,128)(2,1)}, bf16[4,4,200,1024]{3,2,1,0:T(8,128)(2,1)}, bf16[4,4,2,32,3200]{4,3,2,1,0:T(8,128)(2,1)}) custom-call(bf16[2048,1024]{1,0:T(8,128)(2,1)} %get-tuple-element.29.refs_0_, bf16[1024,3200]{1,0:T(8,128)(2,1)} %bitcast.49, bf16[1024,3200]{1,0:T(8,128)(2,1)} %bitcast.51, ...), custom_call_target="tpu_custom_call" | custom-call | tf_op jit(solution)/shard_map/gate_up/pallas_call | solution.py:391
  114.8 50.9 %down.1 = (bf16[2048,1024]{1,0:T(8,128)(2,1)}, bf16[2048,1024]{1,0:T(8,128)(2,1)}, bf16[4,4,2,32,3200]{4,3,2,1,0:T(8,128)(2,1)}, bf16[4,4,200,1024]{3,2,1,0:T(8,128)(2,1)}) custom-call(bf16[2048,3200]{1,0:T(8,128)(2,1)} %get-tuple-element.32.refs_0_, bf16[2048,1024]{1,0:T(8,128)(2,1)} %bitcast.37, bf16[3200,1024]{1,0:T(8,128)(2,1)} %bitcast.47, ...), custom_call_target="tpu_custom_call" | custom-call | tf_op jit(solution)/shard_map/down/pallas_call | solution.py:391
  165.8 56.7 %middle.1 = (bf16[2,2048,3200]{2,1,0:T(8,128)(2,1)}, bf16[2048,3200]{1,0:T(8,128)(2,1)}) custom-call(bf16[2048,1024]{1,0:T(8,128)(2,1)} %get-tuple-element.34.refs_0_, bf16[2048,1024]{1,0:T(8,128)(2,1)} %bitcast.33, bf16[1024,3200]{1,0:T(8,128)(2,1)} %bitcast.39, bf16[1024,3200]{1,0:T(8,128)(2,1)} %bitcast.41, bf16[3200,1024]{1,0:T(8,128)(2,1)} %bitcast.55), custom_call_target="tpu_custom_call" | custom-call | tf_op jit(solution)/shard_map/middle/pallas_call | solution.py:391
  222.4 18.6 %grad_down.2 = bf16[3200,1024]{1,0:T(8,128)(2,1)} custom-call(bf16[2048,3200]{1,0:T(8,128)(2,1)} %get-tuple-element.40.refs_0_, bf16[2048,1024]{1,0:T(8,128)(2,1)} %bitcast.34), custom_call_target="tpu_custom_call" | custom-call | tf_op jit(solution)/shard_map/grad_down/pallas_call | solution.py:391
  241.1 48.6 %grad_gate_up.2 = (bf16[2,1024,3200]{2,1,0:T(8,128)(2,1)}, bf16[200,512]{1,0:T(8,128)(2,1)}) custom-call(bf16[2048,1024]{1,0:T(8,128)(2,1)} %get-tuple-element.34.refs_0_, bf16[2,2048,3200]{2,1,0:T(8,128)(2,1)} %get-tuple-element.38.refs_1_.refs_0_, bf16[4,4,200,1024]{3,2,1,0:T(8,128)(2,1)} %bitcast.46), custom_call_target="tpu_custom_call" | custom-call | tf_op jit(solution)/shard_map/grad_gate_up/pallas_call | solution.py:391
  289.7 10.6 %fusion.3 = (bf16[1,1024,3200]{2,1,0:T(8,128)(2,1)}, bf16[1,1024,3200]{2,1,0:T(8,128)(2,1)}) fusion(bf16[2,1024,3200]{2,1,0:T(8,128)(2,1)} %get-tuple-element.41), kind=kLoop, calls=%fused_computation.19 | loop fusion | bytes 26214400 | tf_op jit(solution)/shard_map/slice | solution.py:603
  300.3 50.6 %input_back.2 = (bf16[2048,1024]{1,0:T(8,128)(2,1)}, bf16[32,3200]{1,0:T(8,128)(2,1)}) custom-call(bf16[2,2048,3200]{2,1,0:T(8,128)(2,1)} %get-tuple-element.38.refs_1_.refs_0_, bf16[1024,3200]{1,0:T(8,128)(2,1)} %bitcast.40, bf16[1024,3200]{1,0:T(8,128)(2,1)} %bitcast.42, bf16[2048,1024]{1,0:T(8,128)(2,1)} %get-tuple-element.39.refs_3_, ...), custom_call_target="tpu_custom_call" | custom-call | tf_op jit(solution)/shard_map/input_back/pallas_call | solution.py:391
  351.0 18.6 %grad_down.3 = bf16[3200,1024]{1,0:T(8,128)(2,1)} custom-call(bf16[2048,3200]{1,0:T(8,128)(2,1)} %get-tuple-element.32.refs_0_, bf16[2048,1024]{1,0:T(8,128)(2,1)} %get-tuple-element.42.refs_0_.refs_1_.refs_4_), custom_call_target="tpu_custom_call" | custom-call | tf_op jit(solution)/shard_map/grad_down/pallas_call | solution.py:391
  369.6 48.4 %hidden_back.1 = (bf16[2,2048,3200]{2,1,0:T(8,128)(2,1)}, bf16[32,3200]{1,0:T(8,128)(2,1)}) custom-call(bf16[2048,1024]{1,0:T(8,128)(2,1)} %get-tuple-element.42.refs_0_.refs_1_.refs_4_, f32[2048,3200]{1,0:T(8,128)} %get-tuple-element.43.refs_1_, f32[2048,3200]{1,0:T(8,128)} %get-tuple-element.44.refs_2_, bf16[3200,1024]{1,0:T(8,128)(2,1)} %bitcast.48, ...), custom_call_target="tpu_custom_call" | custom-call | tf_op jit(solution)/shard_map/hidden_back/pallas_call | solution.py:391
  418.0 49.7 %grad_gate_up.3 = (bf16[2,1024,3200]{2,1,0:T(8,128)(2,1)}, bf16[200,512]{1,0:T(8,128)(2,1)}) custom-call(bf16[2048,1024]{1,0:T(8,128)(2,1)} %get-tuple-element.29.refs_0_, bf16[2,2048,3200]{2,1,0:T(8,128)(2,1)} %get-tuple-element.45.refs_1_.refs_0_, bf16[4,4,200,1024]{3,2,1,0:T(8,128)(2,1)} %bitcast.44), custom_call_target="tpu_custom_call" | custom-call | tf_op jit(solution)/shard_map/grad_gate_up/pallas_call | solution.py:391
  467.6 0.0 copy-start.1
  467.6 0.0 copy-start.2
  467.6 10.7 %fusion.2 = (bf16[1,1024,3200]{2,1,0:T(8,128)(2,1)}, bf16[1,1024,3200]{2,1,0:T(8,128)(2,1)}) fusion(bf16[2,1024,3200]{2,1,0:T(8,128)(2,1)} %get-tuple-element.46), kind=kLoop, calls=%fused_computation.18 | loop fusion | bytes 26214400 | tf_op jit(solution)/shard_map/slice | solution.py:607
  478.3 0.0 copy-done.1
  478.3 0.0 copy-done.2
  478.3 0.1 fusion.1
  478.4 1.3 collective-permute-start.1
  479.7 62.9 %input_back.3 = (bf16[2048,1024]{1,0:T(8,128)(2,1)}, bf16[32,3200]{1,0:T(8,128)(2,1)}, bf16[32,3200]{1,0:T(8,128)(2,1)}) custom-call(bf16[2,2048,3200]{2,1,0:T(8,128)(2,1)} %get-tuple-element.45.refs_1_.refs_0_, bf16[1024,3200]{1,0:T(8,128)(2,1)} %bitcast.50, bf16[1024,3200]{1,0:T(8,128)(2,1)} %bitcast.52, bf16[2048,1024]{1,0:T(8,128)(2,1)} %bitcast.38, ...), custom_call_target="tpu_custom_call" | custom-call | tf_op jit(solution)/shard_map/input_back/pallas_call | solution.py:391
  542.6 0.0 copy-done
  542.6 1.7 pad_maximum_fusion
  544.3 1.8 pad_maximum_fusion.1
  546.1 0.0 collective-permute-done.1
  546.1 0.1 maximum_select_fusion
  546.3 1.2 copy.11
  547.4 4.6 copy.15
  (3 shorter events, 0.1 us)
Async XLA Ops:
  2.0 52.1 %collective-permute-start = (bf16[2,100,512]{2,1,0:T(8,128)(2,1)S(1)}, bf16[2,100,512]{2,1,0:T(8,128)(2,1)S(1)}, u32[]{:S(2)}, u32[]{:S(2)}) collective-permute-start(bf16[2,100,512]{2,1,0:T(8,128)(2,1)S(1)} %copy.13), channel_id=1, source_target_pairs={{0,1},{1,0},{2,3},{3,2},{4,5},{5,4},{6,7},{7,6},{8,9},{9,8},{10,11... | collective-permute-start | bytes 614408 | tf_op jit(solution)/shard_map/ppermute | solution.py:587
  467.6 10.7 %copy-start.1 = (bf16[200,512]{1,0:T(8,128)(2,1)S(1)}, bf16[200,512]{1,0:T(8,128)(2,1)}, u32[]{:S(2)}) copy-start(bf16[200,512]{1,0:T(8,128)(2,1)} %get-tuple-element.53) | copy-start | bytes 614404
  467.6 10.7 %copy-start.2 = (bf16[200,512]{1,0:T(8,128)(2,1)S(1)}, bf16[200,512]{1,0:T(8,128)(2,1)}, u32[]{:S(2)}) copy-start(bf16[200,512]{1,0:T(8,128)(2,1)} %get-tuple-element.52) | copy-start | bytes 614404
  478.4 67.7 %collective-permute-start.1 = (bf16[2,100,512]{2,1,0:T(8,128)(2,1)S(1)}, bf16[2,100,512]{2,1,0:T(8,128)(2,1)S(1)}, u32[]{:S(2)}, u32[]{:S(2)}) collective-permute-start(bf16[2,100,512]{2,1,0:T(8,128)(2,1)S(1)} %get-tuple-element.63), channel_id=1, source_target_pairs={{0,1},{1,0},{2,3},{3,2},{4,5},{5,4},{6,7},{7,6},{8,9},{9,8},{10,11... | collective-permute-start | bytes 614408 | tf_op jit(solution)/shard_map/ppermute | solution.py:612
  479.7 62.9 %copy-start = (bf16[32,3200]{1,0:T(8,128)(2,1)S(1)}, bf16[32,3200]{1,0:T(8,128)(2,1)}, u32[]{:S(2)}) copy-start(bf16[32,3200]{1,0:T(8,128)(2,1)} %get-tuple-element.49) | copy-start | bytes 614404

commit v2 on v1

--- a/solution.py
+++ b/solution.py
@@ -14,6 +14,8 @@
 RING = 4
 EPS = 1e-6
 BM = 256
+CHUNK = 1024
+GRAD_ROWS = 256
 VMEM_LIMIT = 66_000_000
 
 
@@ -116,7 +118,7 @@
 
 
 class Gather:
-    N = 24
+    N = 48
 
     def __init__(self, piece):
         self.piece = piece
@@ -135,10 +137,10 @@
         def of_colour(colour):
             p, q = here.pq(colour)
             p1, pm, q1, qm = ahead(p, 1), ahead(p, RING - 1), ahead(q, 1), ahead(q, RING - 1)
-            q2 = ahead(q, 2)
+            p2, q2 = ahead(p, 2), ahead(q, 2)
             at = functools.partial(piece.of_whole, whole, core, colour)
             dev = functools.partial(here.device, colour)
-            base = 12 * colour
+            base = 24 * colour
 
             def add(name, k, src, dst, device):
                 out[name, colour] = lambda: remote(src(), dst(), self.sems, base + k, device)
@@ -148,12 +150,14 @@
             add("s1-", 1, mine, lambda: at(p, q), dev(pm, q))
             add("s2+", 2, lambda: at(pm, q, 0), lambda: at(pm, q, 0), dev(p1, q))
             add("s2-", 3, lambda: at(p1, q, 1), lambda: at(p1, q, 1), dev(pm, q))
-            add("s3+", 4, lambda: at(ALL, q), lambda: at(ALL, q), dev(p, q1))
-            add("s3-", 5, lambda: at(ALL, q), lambda: at(ALL, q), dev(p, qm))
-            add("s4+", 6, lambda: at(ALL, qm, 0), lambda: at(ALL, qm, 0), dev(p, q1))
-            add("s4-", 7, lambda: at(ALL, q1, 1), lambda: at(ALL, q1, 1), dev(p, qm))
-            for k, of in ((8, q), (9, qm), (10, q1), (11, q2)):
-                add(f"d{k}", k, lambda of=of: at(ALL, of), lambda of=of: at(ALL, of), here.peer())
+            for k, (name, of) in enumerate((("own", p), ("before", pm), ("after", p1), ("far", p2))):
+                src = mine if k == 0 else lambda of=of: at(of, q)
+                add(f"{name}+", 4 + 4 * k, src, lambda of=of: at(of, q), dev(p, q1))
+                add(f"{name}-", 5 + 4 * k, src, lambda of=of: at(of, q), dev(p, qm))
+                add(f"{name} on+", 6 + 4 * k, lambda of=of: at(of, qm, 0), lambda of=of: at(of, qm, 0), dev(p, q1))
+                add(f"{name} on-", 7 + 4 * k, lambda of=of: at(of, q1, 1), lambda of=of: at(of, q1, 1), dev(p, qm))
+            for k, of in enumerate((q, qm, q1, q2)):
+                add(f"d{k}", 20 + k, lambda of=of: at(ALL, of), lambda of=of: at(ALL, of), here.peer())
 
         of_colour(0)
         of_colour(1)
@@ -169,35 +173,39 @@
             self.own, self.piece.chip_of_core(self.whole, here.core, here.x, here.y), self.local
         )
         if stage == 0:
-            start("s1+", "s1-")
+            start("s1+", "s1-", "own+", "own-")
             local().start()
         elif stage == 1:
             for name, then in (("s1+", "s2+"), ("s1-", "s2-")):
                 arrived(name)
                 start(then)
+            start("before+", "before-", "after+", "after-")
         elif stage == 2:
+            for name in ("own+", "own-"):
+                arrived(name)
+                start(f"{name[:-1]} on{name[-1]}")
+            arrived("s2+", "s2-")
+            start("far+", "far-")
             local().wait()
-            arrived("s2+", "s2-")
-            start("s3+", "s3-", "d8")
+            start("d0")
         elif stage == 3:
-            for name, then, peer in (("s3+", "s4+", "d9"), ("s3-", "s4-", "d10")):
+            for name in ("before+", "before-", "after+", "after-"):
                 arrived(name)
-                start(then, peer)
+                start(f"{name[:-1]} on{name[-1]}")
         elif stage == 4:
-            arrived("s4+", "s4-")
-            start("d11")
+            for name, peer in (("far+", "d1"), ("far-", "d2")):
+                arrived(name)
+                start(f"{name[:-1]} on{name[-1]}", peer)
         else:
-            arrived("d8", "d9", "d10", "d11")
+            arrived(*(f"{name} on{way}" for name in ("own", "before", "after", "far") for way in "+-"))
+            start("d3")
+            arrived("d0", "d1", "d2", "d3")
             both([n for n, colour in c if colour == 0], lambda d: d.wait_send())
 
-    STAGES = 6
-
 
 class Scatter:
-    STAGES = 6
-
-    def __init__(self, piece):
-        self.piece = piece
+    def __init__(self, piece, which):
+        self.piece, self.which = piece, which
 
     def scratch(self):
         piece = self.piece
@@ -215,7 +223,7 @@
         ]
 
     def bind(self, terms, result, *scratch):
-        self.terms, self.result = terms, result
+        self.terms, self.result = terms if self.which is None else terms.at[self.which], result
         self.t, self.r, *self.landing, self.acc, send, recv, self.local = scratch
         self.sems = (send, recv)
         return self
@@ -321,8 +329,29 @@
             both([n for n, colour in c if colour == 0], lambda d: d.wait_send())
 
 
-def kernel_call(name, grid, compute, inputs, outputs, parts=1, gathers=(), scatters=(), at=None, collective_id=None, scratch=()):
-    comms = [Gather(p) for p, _ in gathers] + [Scatter(p) for p, _ in scatters]
+class Resident:
+    def __init__(self, array, axis, size, outer=1):
+        self.array, self.axis, self.outer = array, axis, outer
+        self.parts = chunks(array.shape[axis], size)
+
+    def scratch(self):
+        return [pltpu.VMEM(self.array.shape, self.array.dtype), pltpu.SemaphoreType.DMA((self.outer * len(self.parts),))]
+
+    def bind(self, hbm, vmem, sems):
+        self.hbm, self.vmem, self.sems = hbm, vmem, sems
+        return self
+
+    def copy(self, w, j):
+        index = [ALL] * len(self.array.shape)
+        index[self.axis] = pl.ds(*self.parts[j])
+        if self.outer > 1:
+            index[0] = w
+        index = tuple(index)
+        return pltpu.make_async_copy(self.hbm.at[index], self.vmem.at[index], self.sems.at[w * len(self.parts) + j])
+
+
+def kernel_call(name, grid, compute, inputs, outputs, resident=(), parts=1, gathers=(), scatters=(), at=None, collective_id=None):
+    comms = [Gather(p) for p, _ in gathers] + [Scatter(p, w) for p, _, w in scatters]
     n_in, n_out = len(inputs), len(outputs)
     steps = math.prod(grid)
     any_space = pl.BlockSpec(memory_space=pltpu.HBM)
@@ -333,38 +362,48 @@
             return in_vmem(block)
         return pl.BlockSpec(block, index)
 
-    in_specs = [spec(b, i) for _, b, i in inputs]
+    in_specs = [spec(b, i) for _, b, i in inputs] + [any_space] * len(resident)
     out_specs = [spec(b, i) for *_, b, i in outputs]
     out_shape = [jax.ShapeDtypeStruct(s, d) for s, d, *_ in outputs]
-    args = [a for a, *_ in inputs]
+    args = [a for a, *_ in inputs] + [r.array for r in resident]
     for piece, own in gathers:
         args.append(own)
         in_specs.append(in_vmem(own.shape))
         out_shape.append(jax.ShapeDtypeStruct(piece.whole_shape(), BF16))
         out_specs.append(any_space)
-    for piece, terms in scatters:
+    for piece, terms, _ in scatters:
         args.append(terms)
         in_specs.append(any_space)
         shape = (piece.rows, piece.columns)
         out_shape.append(jax.ShapeDtypeStruct(shape, BF16))
         out_specs.append(in_vmem(shape))
+    held = [r.scratch() for r in resident]
     comm_scratch = [c.scratch() for c in comms]
-    scratch_shapes = [*scratch, *(s for group in comm_scratch for s in group)]
+    scratch_shapes = [s for group in held + comm_scratch for s in group]
     last = steps * parts
-    if comms and at is None:
-        at = [min(last, k * last // 6) for k in range(6)]
+    at = at or tuple(k * last // 6 for k in range(6))
 
     def body(*refs):
         refs = list(refs)
         take = lambda n: [refs.pop(0) for _ in range(n)]
-        ins, comm_in = take(n_in), take(len(comms))
+        ins, res_in, comm_in = take(n_in), take(len(resident)), take(len(comms))
         outs, comm_out = take(n_out), take(len(comms))
-        own_scratch = take(len(scratch))
+        for r, i in zip(resident, res_in):
+            r.bind(i, *take(2))
         for comm, i, o, s in zip(comms, comm_in, comm_out, comm_scratch):
             comm.bind(i, o, *take(len(s)))
         step = pl.program_id(0)
         for d in range(1, len(grid)):
             step = step * grid[d] + pl.program_id(d)
+
+        if resident:
+            @pl.when(step == 0)
+            def _():
+                for w in range(max(r.outer for r in resident)):
+                    for j in range(max(len(r.parts) for r in resident)):
+                        for r in resident:
+                            if w < r.outer and j < len(r.parts):
+                                r.copy(w, j).start()
 
         def act(slot):
             if slot == 0:
@@ -375,13 +414,17 @@
                         comm.run(k)
 
         def hook(part):
-            if not comms:
-                return
-            for slot in sorted({0, *at}):
-                if slot < last and slot % parts == part:
-                    pl.when(step == slot // parts)(functools.partial(act, slot))
-
-        compute(hook, step, ins, outs, own_scratch)
+            if comms:
+                for slot in sorted({0, *at}):
+                    if slot < last and slot % parts == part:
+                        pl.when(step == slot // parts)(functools.partial(act, slot))
+
+        def ready(j, *which):
+            for r in which:
+                for w in range(r.outer):
+                    pl.when(step == w * (steps // r.outer))(lambda: r.copy(w, j).wait())
+
+        compute(hook, ready, ins, outs)
         if comms and any(a == last for a in at):
             pl.when(step == steps - 1)(functools.partial(act, last))
 
@@ -398,7 +441,8 @@
     return lax.dot_general(a, b, (((ca,), (cb,)), ((), ())), preferred_element_type=F32)
 
 
-def chunks(n, size=512):
+def chunks(n, size=None):
+    size = size or CHUNK
     return [(i, min(size, n - i)) for i in range(0, n, size)]
 
 
@@ -427,7 +471,8 @@
     return ((dh * u) * (s + silu * (1.0 - s))).astype(BF16), (dh * silu).astype(BF16)
 
 
-def rows_of(array, bm=BM):
+def rows_of(array, bm=None):
+    bm = bm or BM
     block = (bm, *array.shape[1:])
     return array, block, lambda i: (i, 0)
 
@@ -439,7 +484,7 @@
 def k_norm(x, **comm):
     t, d = x.shape
 
-    def compute(hook, step, ins, outs, _):
+    def compute(hook, ready, ins, outs):
         hook(0)
         outs[0][...] = normed(ins[0][...])
 
@@ -449,27 +494,50 @@
 
 def k_gate_up(a, wg, wu, **comm):
     t, f = a.shape[0], wg.shape[1]
-
-    def compute(hook, step, ins, outs, _):
-        a, wg, wu = ins
+    wg, wu = Resident(wg, 1, f), Resident(wu, 1, f)
+
+    def compute(hook, ready, ins, outs):
         g_out, u_out, h_out = outs
-        x = a[...]
+        x = ins[0][...]
         hook(0)
-        for lo, n in chunks(f):
+        ready(0, wg)
+        g_out[...] = dot(x, wg.vmem[...])
+        hook(1)
+        ready(0, wu)
+        u = dot(x, wu.vmem[...])
+        u_out[...] = u
+        h_out[...] = gated(g_out[...], u)
+
+    o = lambda dt: ((t, f), dt, (BM, f), lambda i: (i, 0))
+    return kernel_call(
+        "gate_up", (t // BM,), compute, [rows_of(a)], [o(F32), o(F32), o(BF16)], resident=[wg, wu], parts=2, **comm
+    )
+
+
+def k_middle(a, dy, wg, wu, wd):
+    t, f = a.shape[0], wg.shape[1]
+
+    def compute(hook, ready, ins, outs):
+        a, dy, wg, wu, wd = ins
+        dgu, h_out = outs
+        x, dy = a[...], dy[...]
+        for lo, n in chunks(f, 512):
             cols = pl.ds(lo, n)
             g, u = dot(x, wg[:, cols]), dot(x, wu[:, cols])
-            g_out[:, cols] = g
-            u_out[:, cols] = u
+            dh = dot(dy, wd[cols, :], 1, 1).astype(BF16).astype(F32)
             h_out[:, cols] = gated(g, u)
-
-    o = lambda dt: ((t, f), dt, (BM, f), lambda i: (i, 0))
-    return kernel_call("gate_up", (t // BM,), compute, [rows_of(a), whole(wg), whole(wu)], [o(F32), o(F32), o(BF16)], **comm)
+            dgu[0, :, cols], dgu[1, :, cols] = gated_back(g, u, dh)
+
+    return kernel_call(
+        "middle", (t // BM,), compute, [rows_of(a), rows_of(dy), whole(wg), whole(wu), whole(wd)],
+        [((2, t, f), BF16, (2, BM, f), lambda i: (0, i, 0)), ((t, f), BF16, (BM, f), lambda i: (i, 0))],
+    )
 
 
 def k_down(h, x, wd, **comm):
     t, d = x.shape
 
-    def compute(hook, step, ins, outs, _):
+    def compute(hook, ready, ins, outs):
         h, x, wd = ins
         hook(0)
         y = x[...] + dot(h[...], wd[...]).astype(BF16)
@@ -480,43 +548,24 @@
     return kernel_call("down", (t // BM,), compute, [rows_of(h), rows_of(x), whole(wd)], [o, o], **comm)
 
 
-def k_middle(a, dy, wg, wu, wd):
-    t, f = a.shape[0], wg.shape[1]
-
-    def compute(hook, step, ins, outs, _):
-        a, dy, wg, wu, wd = ins
-        dgu, h_out = outs
-        x, dy = a[...], dy[...]
-        for lo, n in chunks(f):
-            cols = pl.ds(lo, n)
-            g, u = dot(x, wg[:, cols]), dot(x, wu[:, cols])
-            dh = dot(dy, wd[cols, :], 1, 1).astype(BF16).astype(F32)
-            h_out[:, cols] = gated(g, u)
-            dgu[0, :, cols], dgu[1, :, cols] = gated_back(g, u, dh)
-
-    return kernel_call(
-        "middle", (t // BM,), compute,
-        [rows_of(a), rows_of(dy), whole(wg), whole(wu), whole(wd)],
-        [((2, t, f), BF16, (2, BM, f), lambda i: (0, i, 0)), ((t, f), BF16, (BM, f), lambda i: (i, 0))],
-    )
-
-
 def k_hidden_back(dy, g, u, wd, **comm):
     t, f = g.shape
-
-    def compute(hook, step, ins, outs, _):
-        dy, g, u, wd = ins
+    wd = Resident(wd, 0, CHUNK)
+
+    def compute(hook, ready, ins, outs):
+        dy, g, u = ins
         (dgu,) = outs
-        hook(0)
         x = dy[...]
-        for lo, n in chunks(f):
+        for j, (lo, n) in enumerate(chunks(f)):
+            hook(j)
+            ready(j, wd)
             cols = pl.ds(lo, n)
-            dh = dot(x, wd[cols, :], 1, 1).astype(BF16).astype(F32)
+            dh = dot(x, wd.vmem[cols, :], 1, 1).astype(BF16).astype(F32)
             dgu[0, :, cols], dgu[1, :, cols] = gated_back(g[:, cols], u[:, cols], dh)
 
     return kernel_call(
-        "hidden_back", (t // BM,), compute, [rows_of(dy), rows_of(g), rows_of(u), whole(wd)],
-        [((2, t, f), BF16, (2, BM, f), lambda i: (0, i, 0))], **comm,
+        "hidden_back", (t // BM,), compute, [rows_of(dy), rows_of(g), rows_of(u)],
+        [((2, t, f), BF16, (2, BM, f), lambda i: (0, i, 0))], resident=[wd], parts=len(wd.parts), **comm,
     )
 
 
@@ -524,7 +573,7 @@
     (t, f), d = h.shape, dy.shape[1]
     bn = f // 5
 
-    def compute(hook, step, ins, outs, _):
+    def compute(hook, ready, ins, outs):
         hook(0)
         outs[0][...] = dot(ins[0][...], ins[1][...], 0, 0).astype(BF16)
 
@@ -536,37 +585,42 @@
 
 def k_grad_gate_up(a, dgu, **comm):
     (t, d), f = a.shape, dgu.shape[2]
-    bm = d // 4
-
-    def compute(hook, step, ins, outs, _):
-        a, dgu = ins
-        x = a[...]
-        hook(0)
-        for lo, n in chunks(f):
+    bm = GRAD_ROWS
+    dgu = Resident(dgu, 2, f, outer=2)
+
+    def compute(hook, ready, ins, outs):
+        x = ins[0][...]
+        w = pl.program_id(0)
+        for j, (lo, n) in enumerate(chunks(f, f)):
+            hook(j)
+            ready(j, dgu)
             cols = pl.ds(lo, n)
-            outs[0][0, :, cols] = dot(x, dgu[0, :, cols], 0, 0).astype(BF16)
+            outs[0][0, :, cols] = dot(x, dgu.vmem[w, :, cols], 0, 0).astype(BF16)
 
     return kernel_call(
-        "grad_gate_up", (2, 4), compute,
-        [(a, (t, bm), lambda w, i: (0, i)), (dgu, (1, t, f), lambda w, i: (w, 0, 0))],
-        [((2, d, f), BF16, (1, bm, f), lambda w, i: (w, i, 0))], **comm,
+        "grad_gate_up", (2, d // bm), compute, [(a, (t, bm), lambda w, i: (0, i))],
+        [((2, d, f), BF16, (1, bm, f), lambda w, i: (w, i, 0))], resident=[dgu], parts=len(dgu.parts), **comm,
     )
 
 
 def k_input_back(dgu, wg, wu, x, dy, **comm):
     t, d = x.shape
     f = dgu.shape[2]
-
-    def compute(hook, step, ins, outs, _):
-        dgu, wg, wu, x, dy = ins
+    wg, wu = Resident(wg, 0, d), Resident(wu, 0, d)
+
+    def compute(hook, ready, ins, outs):
+        dgu, x, dy = ins
         hook(0)
-        da = dot(dgu[0], wg[...], 1, 1).astype(BF16) + dot(dgu[1], wu[...], 1, 1).astype(BF16)
+        ready(0, wg)
+        by_g = dot(dgu[0], wg.vmem[...], 1, 1).astype(BF16)
+        hook(1)
+        ready(0, wu)
+        da = by_g + dot(dgu[1], wu.vmem[...], 1, 1).astype(BF16)
         outs[0][...] = norm_back(x[...], da, dy[...])
 
     return kernel_call(
-        "input_back", (t // BM,), compute,
-        [(dgu, (2, BM, f), lambda i: (0, i, 0)), whole(wg), whole(wu), rows_of(x), rows_of(dy)],
-        [((t, d), BF16, (BM, d), lambda i: (i, 0))], **comm,
+        "input_back", (t // BM,), compute, [(dgu, (2, BM, f), lambda i: (0, i, 0)), rows_of(x), rows_of(dy)],
+        [((t, d), BF16, (BM, d), lambda i: (i, 0))], resident=[wg, wu], parts=2, **comm,
     )
 
 
@@ -587,24 +641,33 @@
         other = lax.ppermute(lax.dynamic_slice_in_dim(w_down, (1 - core) * half, half, 2), "dp", swap)
         down = jnp.where(core == 0, jnp.concatenate([keep, other], 1), jnp.concatenate([other, keep], 1))
 
-        a0, wg0, wu0 = k_norm(x, gathers=[(row, w_gate[0]), (row, w_up[0])], collective_id=0)
+        a0, wg0, wu0 = k_norm(x, gathers=[(row, w_gate[0]), (row, w_up[0])], at=(0, 4, 5, 6, 7, 8), collective_id=0)
         wg0, wu0 = square(wg0), square(wu0)
-        g0, u0, h0, wd0, wg1 = k_gate_up(a0, wg0, wu0, gathers=[(col, down[0]), (row, w_gate[1])], collective_id=1)
+        g0, u0, h0, wd0, wg1 = k_gate_up(
+            a0, wg0, wu0, gathers=[(col, down[0]), (row, w_gate[1])], at=(0, 3, 6, 10, 13, 16), collective_id=1
+        )
         wd0, wg1 = square(wd0), square(wg1)
-        x1, a1, wu1, wd1 = k_down(h0, x, wd0, gathers=[(row, w_up[1]), (col, down[1])], collective_id=2)
+        x1, a1, wu1, wd1 = k_down(
+            h0, x, wd0, gathers=[(row, w_up[1]), (col, down[1])], at=(0, 3, 5, 8, 8, 8), collective_id=2
+        )
         wu1, wd1 = square(wu1), square(wd1)
 
-        as_row = lambda g: g.reshape(RING, RING, 2, rows, f)
+        as_row = lambda g: g.reshape(2, RING, RING, 2, rows, f)
         as_col = lambda g: g.reshape(RING, RING, 2 * deep, d)
         dgu1, h1 = k_middle(a1, dy, wg1, wu1, wd1)
         (gd1,) = k_grad_down(h1, dy)
-        ggu1, by_d1 = k_grad_gate_up(a1, dgu1, scatters=[(col, as_col(gd1))], collective_id=3)
-        dx1, by_g1 = k_input_back(dgu1, wg1, wu1, x1, dy, scatters=[(row, as_row(ggu1[0]))], collective_id=4)
-        dgu0, by_u1 = k_hidden_back(dx1, g0, u0, wd0, scatters=[(row, as_row(ggu1[1]))], collective_id=5)
+        ggu1, by_d1 = k_grad_gate_up(a1, dgu1, scatters=[(col, as_col(gd1), None)], at=(0, 2, 4, 7, 8, 8), collective_id=3)
+        dx1, by_g1 = k_input_back(
+            dgu1, wg1, wu1, x1, dy, scatters=[(row, as_row(ggu1), 0)], at=(0, 4, 8, 13, 15, 16), collective_id=4
+        )
         (gd0,) = k_grad_down(h0, dx1)
-        ggu0, by_d0 = k_grad_gate_up(a0, dgu0, scatters=[(col, as_col(gd0))], collective_id=6)
+        dgu0, by_u1 = k_hidden_back(
+            dx1, g0, u0, wd0, scatters=[(row, as_row(ggu1), 1)], at=(0, 7, 15, 27, 31, 32), collective_id=5
+        )
+        ggu0, by_d0 = k_grad_gate_up(a0, dgu0, scatters=[(col, as_col(gd0), None)], at=(0, 2, 4, 7, 8, 8), collective_id=6)
         by_x, by_g0, by_u0 = k_input_back(
-            dgu0, wg0, wu0, x, dx1, scatters=[(row, as_row(ggu0[0])), (row, as_row(ggu0[1]))], collective_id=7
+            dgu0, wg0, wu0, x, dx1, scatters=[(row, as_row(ggu0), 0), (row, as_row(ggu0), 1)],
+            at=(0, 5, 10, 16, 16, 16), collective_id=7,
         )
 
         by_down = jnp.stack([by_d0, by_d1])

time: 560 us -> 502 us (0.90)
  Pallas kernels: 513 us -> 473 us
  local copies, waits for them, and re-layouts: 31.4 us -> 10.1 us
    pallas_call x11, Pallas kernels: 513 us -> 473 us  [kernel_call(): pl.pallas_call(body, grid=grid, in_specs=in_specs, out_specs=out_specs, o...]
    slice x2 -> x0, local copies, waits for them, and re-layouts: 21.3 us -> none  [the longest x1 10.7 us: step(): ggu0[1]]
  transfers between devices with their start and end apart: 2 -> 2, of which waited for: 0 -> 0; matrix products, arithmetic and copies ran while one was open for 1% -> 1% of each run, Pallas kernels for 20% -> 10%
where the time goes in v2:
time: 502 us; the launch traced here: 495 us
  Pallas kernels  473 us (94%)
  local copies, waits for them, and re-layouts  10.1 us (2%)
  starting transfers between devices  6.18 us (1%)
    pallas_call x11, Pallas kernels, kernel_call(): pl.pallas_call(body, grid=grid, in_specs=in_specs, out_specs=out_specs, o...  473 us
  transfers between devices with their start and end apart: 2, of which 0 were waited for; matrix products, arithmetic and copies ran while one was open for 1% of the time, Pallas kernels for 10%

profile of v2, /device:TPU:97, one launch (start us, length us, event | category | flops | bytes accessed | tf_op | source)
XLA Modules:
  0.0 494.6 jit_solution(15120196770859136682)
XLA Ops:
  0.6 1.3 constant_dynamic-slice_fusion.1
  2.0 2.1 collective-permute-start
  4.1 2.1 slice_bitcast_fusion.2
  6.3 48.6 %norm.1 = (bf16[2048,1024]{1,0:T(8,128)(2,1)}, bf16[4,4,2,32,3200]{4,3,2,1,0:T(8,128)(2,1)}, bf16[4,4,2,32,3200]{4,3,2,1,0:T(8,128)(2,1)}) custom-call(bf16[2048,1024]{1,0:T(8,128)(2,1)} %bitcast.35, bf16[32,3200]{1,0:T(8,128)(2,1)} %get-tuple-element.68.refs_1_, bf16[32,3200]{1,0:T(8,128)(2,1)} %get-tuple-element.63.refs_2_), custom_call_target="tpu_custom_call" | custom-call | tf_op jit(solution)/shard_map/norm/pallas_call | solution.py:434
  54.9 0.0 collective-permute-done
  54.9 0.1 maximum_select_fusion.1
  55.1 0.8 slice_bitcast_fusion
  55.8 51.4 %gate_up.1 = (f32[2048,3200]{1,0:T(8,128)}, f32[2048,3200]{1,0:T(8,128)}, bf16[2048,3200]{1,0:T(8,128)(2,1)}, bf16[4,4,200,1024]{3,2,1,0:T(8,128)(2,1)}, bf16[4,4,2,32,3200]{4,3,2,1,0:T(8,128)(2,1)}) custom-call(bf16[2048,1024]{1,0:T(8,128)(2,1)} %get-tuple-element.29.refs_0_, bf16[1024,3200]{1,0:T(8,128)(2,1)} %bitcast.41, bf16[1024,3200]{1,0:T(8,128)(2,1)} %bitcast.43, ...), custom_call_target="tpu_custom_call" | custom-call | tf_op jit(solution)/shard_map/gate_up/pallas_call | solution.py:434
  107.2 47.6 %down.1 = (bf16[2048,1024]{1,0:T(8,128)(2,1)}, bf16[2048,1024]{1,0:T(8,128)(2,1)}, bf16[4,4,2,32,3200]{4,3,2,1,0:T(8,128)(2,1)}, bf16[4,4,200,1024]{3,2,1,0:T(8,128)(2,1)}) custom-call(bf16[2048,3200]{1,0:T(8,128)(2,1)} %get-tuple-element.32.refs_0_, bf16[2048,1024]{1,0:T(8,128)(2,1)} %bitcast.36, bf16[3200,1024]{1,0:T(8,128)(2,1)} %bitcast.47, ...), custom_call_target="tpu_custom_call" | custom-call | tf_op jit(solution)/shard_map/down/pallas_call | solution.py:434
  154.8 56.2 %middle.1 = (bf16[2,2048,3200]{2,1,0:T(8,128)(2,1)}, bf16[2048,3200]{1,0:T(8,128)(2,1)}) custom-call(bf16[2048,1024]{1,0:T(8,128)(2,1)} %get-tuple-element.34.refs_0_, bf16[2048,1024]{1,0:T(8,128)(2,1)} %bitcast.38, bf16[1024,3200]{1,0:T(8,128)(2,1)} %bitcast.49, bf16[1024,3200]{1,0:T(8,128)(2,1)} %bitcast.51, bf16[3200,1024]{1,0:T(8,128)(2,1)} %bitcast.53), custom_call_target="tpu_custom_call" | custom-call | tf_op jit(solution)/shard_map/middle/pallas_call | solution.py:434
  211.0 18.7 %grad_down.2 = bf16[3200,1024]{1,0:T(8,128)(2,1)} custom-call(bf16[2048,3200]{1,0:T(8,128)(2,1)} %get-tuple-element.40.refs_0_, bf16[2048,1024]{1,0:T(8,128)(2,1)} %bitcast.39), custom_call_target="tpu_custom_call" | custom-call | tf_op jit(solution)/shard_map/grad_down/pallas_call | solution.py:434
  229.7 42.9 %grad_gate_up.2 = (bf16[2,1024,3200]{2,1,0:T(8,128)(2,1)}, bf16[200,512]{1,0:T(8,128)(2,1)}) custom-call(bf16[2048,1024]{1,0:T(8,128)(2,1)} %get-tuple-element.34.refs_0_, bf16[2,2048,3200]{2,1,0:T(8,128)(2,1)} %get-tuple-element.38.refs_1_.refs_0_, bf16[4,4,200,1024]{3,2,1,0:T(8,128)(2,1)} %bitcast.46), custom_call_target="tpu_custom_call" | custom-call | tf_op jit(solution)/shard_map/grad_gate_up/pallas_call | solution.py:434
  272.5 45.6 %input_back.2 = (bf16[2048,1024]{1,0:T(8,128)(2,1)}, bf16[32,3200]{1,0:T(8,128)(2,1)}) custom-call(bf16[2,2048,3200]{2,1,0:T(8,128)(2,1)} %get-tuple-element.38.refs_1_.refs_0_, bf16[2048,1024]{1,0:T(8,128)(2,1)} %get-tuple-element.39.refs_1_, bf16[2048,1024]{1,0:T(8,128)(2,1)} %bitcast.40, bf16[1024,3200]{1,0:T(8,128)(2,1)} %bitcast.50, ...), custom_call_target="tpu_custom_call" | custom-call | tf_op jit(solution)/shard_map/input_back/pallas_call | solution.py:434
  318.1 18.6 %grad_down.3 = bf16[3200,1024]{1,0:T(8,128)(2,1)} custom-call(bf16[2048,3200]{1,0:T(8,128)(2,1)} %get-tuple-element.32.refs_0_, bf16[2048,1024]{1,0:T(8,128)(2,1)} %get-tuple-element.42.refs_0_.refs_1_.refs_2_), custom_call_target="tpu_custom_call" | custom-call | tf_op jit(solution)/shard_map/grad_down/pallas_call | solution.py:434
  336.7 42.0 %hidden_back.1 = (bf16[2,2048,3200]{2,1,0:T(8,128)(2,1)}, bf16[32,3200]{1,0:T(8,128)(2,1)}) custom-call(bf16[2048,1024]{1,0:T(8,128)(2,1)} %get-tuple-element.42.refs_0_.refs_1_.refs_2_, f32[2048,3200]{1,0:T(8,128)} %get-tuple-element.43.refs_1_, f32[2048,3200]{1,0:T(8,128)} %get-tuple-element.44.refs_2_, bf16[3200,1024]{1,0:T(8,128)(2,1)} %bitcast.48, ...), custom_call_target="tpu_custom_call" | custom-call | tf_op jit(solution)/shard_map/hidden_back/pallas_call | solution.py:434
  378.7 44.2 %grad_gate_up.3 = (bf16[2,1024,3200]{2,1,0:T(8,128)(2,1)}, bf16[200,512]{1,0:T(8,128)(2,1)}) custom-call(bf16[2048,1024]{1,0:T(8,128)(2,1)} %get-tuple-element.29.refs_0_, bf16[2,2048,3200]{2,1,0:T(8,128)(2,1)} %get-tuple-element.45.refs_1_.refs_0_, bf16[4,4,200,1024]{3,2,1,0:T(8,128)(2,1)} %bitcast.45), custom_call_target="tpu_custom_call" | custom-call | tf_op jit(solution)/shard_map/grad_gate_up/pallas_call | solution.py:434
  423.0 0.0 copy-start.1
  423.0 0.0 copy-start.3
  423.0 0.0 copy-start
  423.0 0.0 copy-start.2
  423.0 57.5 %input_back.3 = (bf16[2048,1024]{1,0:T(8,128)(2,1)}, bf16[32,3200]{1,0:T(8,128)(2,1)}, bf16[32,3200]{1,0:T(8,128)(2,1)}) custom-call(bf16[2,2048,3200]{2,1,0:T(8,128)(2,1)} %get-tuple-element.45.refs_1_.refs_0_, bf16[2048,1024]{1,0:T(8,128)(2,1)} %bitcast.37, bf16[2048,1024]{1,0:T(8,128)(2,1)} %get-tuple-element.42.refs_0_.refs_1_.refs_2_, ...), custom_call_target="tpu_custom_call" | custom-call | tf_op jit(solution)/shard_map/input_back/pallas_call | solution.py:434
  480.6 0.0 copy-done.1
  480.6 0.0 copy-done.3
  480.6 0.1 fusion.1
  480.7 4.1 collective-permute-start.1
  484.8 0.0 copy-done
  484.8 1.7 pad_maximum_fusion
  486.5 1.7 pad_maximum_fusion.1
  488.2 0.0 collective-permute-done.1
  488.2 0.1 maximum_select_fusion
  488.3 1.2 copy.11
  489.5 4.6 copy.15
  (3 shorter events, 0.1 us)
Async XLA Ops:
  2.0 52.9 %collective-permute-start = (bf16[2,100,512]{2,1,0:T(8,128)(2,1)S(1)}, bf16[2,100,512]{2,1,0:T(8,128)(2,1)S(1)}, u32[]{:S(2)}, u32[]{:S(2)}) collective-permute-start(bf16[2,100,512]{2,1,0:T(8,128)(2,1)S(1)} %copy.13), channel_id=1, source_target_pairs={{0,1},{1,0},{2,3},{3,2},{4,5},{5,4},{6,7},{7,6},{8,9},{9,8},{10,11... | collective-permute-start | bytes 614408 | tf_op jit(solution)/shard_map/ppermute | solution.py:641
  423.0 57.6 %copy-start.1 = (bf16[200,512]{1,0:T(8,128)(2,1)S(1)}, bf16[200,512]{1,0:T(8,128)(2,1)}, u32[]{:S(2)}) copy-start(bf16[200,512]{1,0:T(8,128)(2,1)} %get-tuple-element.53) | copy-start | bytes 614404
  423.0 57.6 %copy-start.3 = (bf16[200,512]{1,0:T(8,128)(2,1)S(1)}, bf16[200,512]{1,0:T(8,128)(2,1)}, u32[]{:S(2)}) copy-start(bf16[200,512]{1,0:T(8,128)(2,1)} %get-tuple-element.52) | copy-start | bytes 614404
  423.0 61.8 %copy-start = (bf16[32,3200]{1,0:T(8,128)(2,1)S(1)}, bf16[32,3200]{1,0:T(8,128)(2,1)}, u32[]{:S(2)}) copy-start(bf16[32,3200]{1,0:T(8,128)(2,1)} %get-tuple-element.49) | copy-start | bytes 614404
  423.0 63.5 %copy-start.2 = (bf16[32,3200]{1,0:T(8,128)(2,1)S(1)}, bf16[32,3200]{1,0:T(8,128)(2,1)}, u32[]{:S(2)}) copy-start(bf16[32,3200]{1,0:T(8,128)(2,1)} %get-tuple-element.51) | copy-start | bytes 614404
  480.7 7.5 %collective-permute-start.1 = (bf16[2,100,512]{2,1,0:T(8,128)(2,1)S(1)}, bf16[2,100,512]{2,1,0:T(8,128)(2,1)S(1)}, u32[]{:S(2)}, u32[]{:S(2)}) collective-permute-start(bf16[2,100,512]{2,1,0:T(8,128)(2,1)S(1)} %get-tuple-element.59), channel_id=1, source_target_pairs={{0,1},{1,0},{2,3},{3,2},{4,5},{5,4},{6,7},{7,6},{8,9},{9,8},{10,11... | collective-permute-start | bytes 614408 | tf_op jit(solution)/shard_map/ppermute | solution.py:675
